TPU v7x, 512 devices: a whole 4x4x16 slice. The times are simulated.
512 devices in a mesh: band: 16 (over z), ga: 32 (over y, x, core).
Axes of the slice: x: 4, y: 4, z: 16, core: 2. Of those that a mesh axis runs over, the one named last changes fastest.
Arguments:
- waves: bfloat16 [2, 512, 32768], P(None, 'band', 'ga'), may hold values from -6 to 6
- occupations: float32 [512], P('band'), may hold values from 0.000390625 to 0.0078125
- beta_table: float32 [72, 32768], P(None, 'ga'), may hold values from -0.0234375 to 0.0234375
- wave_miller: int32 [3, 32768], P(None, 'ga'), may hold values from 0 to 223
- atom_kinds: int32 [256], replicated, may hold values from 0 to 3
- atom_sites: int32 [3, 256], replicated, may hold values from 0 to 223
- aug_table: bfloat16 [684, 917504], P(None, ('band', 'ga')), may hold values from -0.00015258789 to 0.00015258789
- stick_columns: int32 [4096], P(('band', 'ga')), may hold values from -1 to 3599, as said below
Outputs:
- density: float32 [2, 224, 240, 240], P(None, 'ga', 'band')
Inputs may be any that keep to these rules, and one draw needn't show every extreme that they name: `stick_columns`: entry t is a slot of the device at place t // 8 in band-major order, of band index t // 256. -1 marks an empty slot; otherwise the entry c names the column x = (t // 256) * 15 + c // 240, y = c mod 240. Live columns of one band index are distinct. On each device the live slots come first and at least one is live; in each band index some device has all 8 slots live.
All inputs are finite; a program needn't handle non-finite values.
Results may differ from a plain program's by a relative error of at most 0.0035.
Values sent between devices are 32-bit elements; how exact they have to be, the bound alone decides.
A program may use at most 64 MiB of HBM per device.

v0:
```python
import functools

import jax
import jax.numpy as jnp
import numpy as np
from jax import lax
from jax.experimental import pallas as pl
from jax.experimental.pallas import tpu as pltpu
from jax.sharding import PartitionSpec as P

NH = 18
PAIRS = 171
SPECIES = 4
NXB = 15
NPL = 7
STK = 8
OWN_ATOMS = 8
HALF = NH // 2
ROWS = HALF * OWN_ATOMS
DESTS = 4
LANES = 128
KLANES = 768

ELL = [0] * 2 + [1] * 6 + [2] * 10
COS = (0.999999989, -19.7392045, 64.9391175, -85.4501395, 60.167631, -25.9675992, 6.52865816)
SIN = (6.28318492, -41.3415892, 81.5999433, -76.6144725, 41.3428824, -12.4712435)

MESH = pl.DeviceIdType.MESH
F32 = jnp.float32
BF16 = jnp.bfloat16
highest = lax.Precision.HIGHEST


def round_up(value, step):
    return (value + step - 1) // step * step


def cos_sin(turns):
    u = turns - jnp.floor(turns + 0.5)
    w = u * u
    c = COS[-1]
    for a in COS[-2::-1]:
        c = c * w + a
    s = SIN[-1]
    for a in SIN[-2::-1]:
        s = s * w + a
    return c, s * u


def turns_of(product, length):
    inverse = 1.0 / length
    return (product - length * jnp.floor(product * inverse)) * inverse


def split(x):
    hi = x.astype(BF16)
    return hi, (x - hi.astype(F32)).astype(BF16)


def dot_nt(a, b, **kw):
    return lax.dot_general(a, b, (((1,), (1,)), ((), ())), preferred_element_type=F32, **kw)


def dot_nn(a, b, **kw):
    return lax.dot_general(a, b, (((1,), (0,)), ((), ())), preferred_element_type=F32, **kw)


def kernel(
    nb,
    ng,
    gt_lanes,
    waves_ref,
    occ_ref,
    beta_ref,
    mil_ref,
    kinds_ref,
    sites_ref,
    tab_hbm,
    sticks_ref,
    tz_hbm,
    tx_hbm,
    even_ref,
    out_ref,
    tab,
    tz,
    tx,
    local_sem,
    colb,
    mil,
    wmat,
    acc,
    send_p,
    recv_p,
    send_b,
    recv_b,
    send_c,
    recv_c,
    occ_row,
    phase,
    send_z,
    recv_z,
    send_a,
    recv_a,
    wre,
    wim,
    augrow,
    send_v,
    recv_v,
    ey,
    onehot,
    vexp,
    send_y,
    recv_y,
    p_ssem,
    p_rsem,
    b_ssem,
    b_rsem,
    c_ssem,
    c_rsem,
    z_ssem,
    z_rsem,
    a_ssem,
    a_rsem,
    v_ssem,
    v_rsem,
    y_ssem,
    y_rsem,
):
    nx, nz = NXB * nb, NPL * ng
    atoms = OWN_ATOMS * ng
    slots = STK * ng
    band_dev, wave_count = waves_ref.shape[1], waves_ref.shape[2]
    tiles = wave_count // gt_lanes
    steps = ng // 2 // DESTS
    cy = 4 if ng == 32 else 2
    cx = ng // 2 // cy
    columns = STK * nz
    ct = columns // NPL
    b = lax.axis_index("band")
    j = lax.axis_index("ga")
    core = j % 2
    chip = j // 2
    chip_y = chip // cx
    chip_x = chip % cx

    local = [
        pltpu.make_async_copy(tab_hbm, tab, local_sem.at[0]),
        pltpu.make_async_copy(tz_hbm, tz, local_sem.at[1]),
        pltpu.make_async_copy(tx_hbm, tx, local_sem.at[2]),
    ]
    for copy in local:
        copy.start()

    barrier = pltpu.get_barrier_semaphore()

    def greet_ga(k, carry):
        pl.semaphore_signal(barrier, inc=1, device_id=(b, (j + k) % ng), device_id_type=MESH)
        return carry

    def greet_band(k, carry):
        pl.semaphore_signal(barrier, inc=1, device_id=((b + k) % nb, j), device_id_type=MESH)
        return carry

    lax.fori_loop(1, nb, greet_band, 0)
    lax.fori_loop(1, ng, greet_ga, 0)

    cols = jnp.concatenate(
        [
            sites_ref[...].astype(F32),
            kinds_ref[...].astype(F32),
            jnp.zeros((4, atoms), F32),
        ],
        axis=0,
    ).T
    for n in range(4):
        colb[n] = jnp.broadcast_to(cols[:, n : n + 1], (atoms, LANES))
    mil[0:3, :] = mil_ref[...].astype(F32)
    occ_row[...] = jnp.zeros(occ_row.shape, F32)
    occ_row[0:1, 0:band_dev] = occ_ref[...]
    stick = [sticks_ref[t].astype(F32) for t in range(STK)]
    slot_row = lax.broadcasted_iota(jnp.int32, (STK, LANES), 0)
    mine = jnp.zeros((STK, LANES), F32)
    for t in range(STK):
        mine = jnp.where(slot_row == t, stick[t], mine)
    send_c[...] = mine
    recv_c[j] = mine

    width = 2 * band_dev
    for g in range(tiles):
        lanes = slice(g * gt_lanes, (g + 1) * gt_lanes)
        wr = waves_ref[0, :, lanes].astype(F32)
        wi = waves_ref[1, :, lanes].astype(F32)
        none = jnp.zeros((LANES - width, gt_lanes), F32)
        with_cos = jnp.concatenate([wr, wi], axis=0)
        with_sin = jnp.concatenate([-wi, wr], axis=0)
        for h in range(2):
            for n, part in enumerate((with_cos, with_sin)):
                full = jnp.concatenate([part, none] if h == 0 else [none, part], axis=0)
                wmat[g, (2 * h + n) * gt_lanes : (2 * h + n + 1) * gt_lanes, :] = full.T.astype(BF16)

    def wide(x, lanes):
        return jnp.concatenate([x] * (lanes // LANES), axis=1) if lanes > LANES else x[:, :lanes]

    def chip_of(index):
        e = cy * cx - 1 - index
        return ((chip_y + e // cx) % cy) * cx + (chip_x + e % cx) % cx

    def project(step, parity):
        acc[...] = jnp.zeros(acc.shape, F32)

        def tile(g, carry):
            lanes = pl.ds(pl.multiple_of(g * gt_lanes, gt_lanes), gt_lanes)
            m1, m2, m3 = mil[0:1, lanes], mil[1:2, lanes], mil[2:3, lanes]
            parts = [[], [], [], []]
            for d in range(DESTS):
                dest = 2 * chip_of(step * DESTS + d) + parity
                rows = pl.ds(pl.multiple_of(dest * OWN_ATOMS, OWN_ATOMS), OWN_ATOMS)
                p1, p2, p3, kind = (wide(colb[n, rows, :], gt_lanes) for n in range(4))
                turns = turns_of(p1 * m1 + p2 * m2, nx) + turns_of(p3 * m3, nz)
                c, s = cos_sin(turns)
                pair = ((c, s), (-s, c), (-c, -s))
                upper = kind > 1.5
                odd_low = kind > 0.5
                odd_high = kind > 2.5
                for i in range(NH):
                    beta = [beta_ref[n * NH + i : n * NH + i + 1, lanes] for n in range(SPECIES)]
                    radial = jnp.where(
                        upper,
                        jnp.where(odd_high, beta[3], beta[2]),
                        jnp.where(odd_low, beta[1], beta[0]),
                    )
                    first, second = pair[ELL[i]]
                    h = i // HALF
                    parts[2 * h].append(radial * first)
                    parts[2 * h + 1].append(radial * second)
            left = jnp.concatenate([jnp.concatenate(p, axis=0).astype(BF16) for p in parts], axis=1)
            acc[...] += dot_nn(left, wmat[g])
            return carry

        lax.fori_loop(0, tiles, tile, 0)

    def for_partner(step, carry):
        project(step, 1 - core)
        send_p[step] = acc[...]
        return carry

    lax.fori_loop(0, steps, for_partner, 0)
    pl.semaphore_wait(barrier, (nb - 1) + (ng - 1))

    def copy_p(step):
        return pltpu.make_async_remote_copy(
            send_p.at[step],
            recv_p.at[step],
            p_ssem.at[step],
            p_rsem.at[step],
            device_id=(b, chip * 2 + 1 - core),
            device_id_type=MESH,
        )

    def copy_ga(source, target, ssem, rsem, k):
        return pltpu.make_async_remote_copy(
            source,
            target,
            ssem.at[k],
            rsem.at[k],
            device_id=(b, (j + k) % ng),
            device_id_type=MESH,
        )

    def band_offset(k):
        half = nb // 2
        m = (k + 1) // 2
        return half + m * (1 - 2 * (k % 2))

    def copy_band(source, target, ssem, rsem, off):
        return pltpu.make_async_remote_copy(
            source,
            target,
            ssem.at[off],
            rsem.at[off],
            device_id=((b + off) % nb, j),
            device_id_type=MESH,
        )

    def loop(low, high, body):
        def step(k, carry):
            body(k)
            return carry

        lax.fori_loop(low, high, step, 0)

    loop(0, steps, lambda s: copy_p(s).start())
    loop(1, ng, lambda k: copy_ga(send_c, recv_c.at[j], c_ssem, c_rsem, k).start())

    def copy_b(index):
        return pltpu.make_async_remote_copy(
            send_b.at[index],
            recv_b.at[index],
            b_ssem.at[index],
            b_rsem.at[index],
            device_id=(b, 2 * chip_of(index) + core),
            device_id_type=MESH,
        )

    last = cy * cx - 1

    def for_owners(step, carry):
        project(step, core)
        copy_p(step).wait_recv()
        for d in range(DESTS):
            index = step * DESTS + d
            block = acc[d * ROWS : (d + 1) * ROWS, :] + recv_p[step, d * ROWS : (d + 1) * ROWS, :]
            send_b[index] = block

            @pl.when(index < last)
            def _():
                copy_b(index).start()

        return carry

    lax.fori_loop(0, steps, for_owners, 0)

    def phases(t):
        lanes = pl.ds(pl.multiple_of(t * ct, ct), ct)
        g = (lax.broadcasted_iota(jnp.int32, (1, ct), 1) + t * ct).astype(F32)
        slot = jnp.floor((g + 0.5) * (1.0 / nz))
        z = g - slot * nz
        column = jnp.zeros((1, ct), F32)
        for n in range(STK):
            column = jnp.where(slot == n, stick[n], column)
        x = jnp.floor((column + 0.5) * (1.0 / nx))
        y = column - x * nx
        x = x + (b * NXB).astype(F32)

        def row(r):
            rows = pl.ds(pl.multiple_of(r * 8, 8), 8)
            p1, p2, p3 = (wide(colb[n, rows, :], ct) for n in range(3))
            turns = turns_of(p1 * x + p2 * y, nx) + turns_of(p3 * z, nz)
            c, s = cos_sin(turns)
            phase[0, rows, lanes] = c
            phase[1, rows, lanes] = s

        loop(0, atoms // 8, row)

    loop(0, NPL, phases)

    def wait_b(index):
        copy_b(index).wait_recv()

    loop(0, last, wait_b)
    becp = send_b[last]
    for index in range(last):
        becp = becp + recv_b[index]
    occ = occ_row[...]
    occ = sum((pltpu.roll(occ, n * band_dev, 1) for n in range(1, LANES // band_dev)), occ)[0:1]
    lane = lax.broadcasted_iota(jnp.int32, (1, LANES), 1)
    occ = jnp.where(lane < width, occ, 0.0)
    both = jnp.concatenate([becp, pltpu.roll(becp, LANES - width, 1)], axis=0)
    gram = dot_nt(both * occ, both, precision=highest)
    rows = NH * OWN_ATOMS
    row_id = lax.broadcasted_iota(jnp.int32, (rows, rows), 0)
    col_id = lax.broadcasted_iota(jnp.int32, (rows, rows), 1)
    gram = jnp.where(row_id % OWN_ATOMS == col_id % OWN_ATOMS, gram, 0.0)
    pick = (
        lax.broadcasted_iota(jnp.int32, (rows, LANES), 0) // OWN_ATOMS
        == lax.broadcasted_iota(jnp.int32, (rows, LANES), 1)
    ).astype(F32)
    square = dot_nn(gram, pick, precision=highest)
    total = jnp.zeros((OWN_ATOMS, 2 * LANES), F32)
    for i in range(NH):
        factor = jnp.where(lane < i, 0.0, jnp.where(lane == i, 1.0, 2.0))
        factor = jnp.where(lane < NH, factor, 0.0)
        piece = square[i * OWN_ATOMS : (i + 1) * OWN_ATOMS] * factor
        piece = jnp.concatenate([piece, jnp.zeros((OWN_ATOMS, LANES), F32)], axis=1)
        shift = i * NH - i * (i - 1) // 2 - i
        total = total + (pltpu.roll(piece, shift, 1) if shift else piece)
    send_z[...] = total
    recv_z[0] = total

    def send_band(k):
        off = band_offset(k)
        copy_band(send_z, recv_z.at[off], z_ssem, z_rsem, off).start()

    loop(0, nb - 1, send_band)

    loop(1, ng, lambda k: copy_ga(send_c, recv_c.at[j], c_ssem, c_rsem, k).wait_recv())
    column = recv_c[...].reshape(slots, LANES)
    slot_x = jnp.floor((column + 0.5) * (1.0 / nx))
    slot_y = column - slot_x * nx
    hot = (slot_x == lax.broadcasted_iota(jnp.int32, (slots, LANES), 1).astype(F32)).astype(F32)
    onehot[...] = hot.T[0:16].astype(BF16)
    lane_y = (lax.broadcasted_iota(jnp.int32, (1, LANES), 1) % 16).astype(F32)

    def y_phases(n):
        turns = turns_of(slot_y * (lane_y + (n * NXB).astype(F32)), nx)
        c, s = cos_sin(turns)
        ey[n, 0] = c
        ey[n, 1] = s

    loop(0, nb, y_phases)

    def wait_band(k):
        off = band_offset(k)
        copy_band(send_z, recv_z.at[off], z_ssem, z_rsem, off).wait_recv()

    loop(0, nb - 1, wait_band)
    total = recv_z[0]
    for n in range(1, nb):
        total = total + recv_z[n]
    send_a[...] = total
    recv_a[j] = total
    loop(1, ng, lambda k: copy_ga(send_a, recv_a.at[j], a_ssem, a_rsem, k).start())
    for copy in local:
        copy.wait()
    loop(1, ng, lambda k: copy_ga(send_a, recv_a.at[j], a_ssem, a_rsem, k).wait_recv())

    even = even_ref[0:1, :]
    odd = even_ref[1:2, :]

    def weights(r):
        values = recv_a[pl.ds(2 * r, 2)].reshape(16, 2 * LANES)
        values = jnp.concatenate([values, jnp.zeros((16, KLANES - 2 * LANES), F32)], axis=1)
        rows = pl.ds(pl.multiple_of(r * 16, 16), 16)
        kind = wide(colb[3, rows, :], KLANES)
        placed = jnp.where(kind < 0.5, values, 0.0)
        for n in range(1, SPECIES):
            moved = pltpu.roll(values, n * PAIRS, 1)
            placed = jnp.where((kind > n - 0.5) & (kind < n + 0.5), moved, placed)
        wre[rows, :] = (placed * even).astype(BF16)
        wim[rows, :] = (placed * odd).astype(BF16)

    loop(0, atoms // 16, weights)
    depth = SPECIES * PAIRS

    def coefficients(t):
        lanes = pl.ds(pl.multiple_of(t * ct, ct), ct)
        table = tab[:, lanes]
        amp_re = dot_nn(wre[:, :depth], table)
        amp_im = dot_nn(wim[:, :depth], table)
        c, s = phase[0, :, lanes], phase[1, :, lanes]
        augrow[0:1, lanes] = jnp.sum(amp_re * c + amp_im * s, axis=0, keepdims=True)
        augrow[1:2, lanes] = jnp.sum(amp_im * c - amp_re * s, axis=0, keepdims=True)

    loop(0, NPL, coefficients)

    pad_z = tz.shape[2] // 2
    wide_row = round_up(columns, LANES)
    shape = (STK, pad_z)
    slot_id = lax.broadcasted_iota(jnp.int32, shape, 0)
    lane_id = lax.broadcasted_iota(jnp.int32, shape, 1)
    values = []
    for n in range(2):
        row = augrow[n : n + 1, :]
        picked = jnp.zeros(shape, F32)
        for t in range(STK):
            moved = pltpu.roll(row, wide_row - t * nz, 1) if t else row
            picked = jnp.where(slot_id == t, moved[:, :pad_z], picked)
        values.append(jnp.where(lane_id < nz, picked, 0.0))
    a_re, a_im = values
    pair = jnp.concatenate(
        [jnp.concatenate([a_re, -a_im], axis=1), jnp.concatenate([a_im, a_re], axis=1)], axis=0
    )
    group = lax.broadcasted_iota(jnp.int32, (LANES, 1), 0) // (2 * STK)
    placed = jnp.where(group == j % 8, jnp.concatenate([pair] * 8, axis=0), 0.0)
    hi, lo = split(placed)
    planes = dot_nt(tz[0], hi) + dot_nt(tz[0], lo) + dot_nt(tz[1], hi)
    send_v[...] = planes.reshape(ng, 8, LANES)
    recv_v[j] = send_v[j]

    def copy_v(k):
        return copy_ga(send_v.at[(j + k) % ng], recv_v.at[j], v_ssem, v_rsem, k)

    loop(1, ng, lambda k: copy_v(k).start())
    loop(1, ng, lambda k: copy_v(k).wait_recv())

    groups = max(ng // 8, 1)
    expand = (
        lax.broadcasted_iota(jnp.int32, (8, LANES), 1) // 16
        == lax.broadcasted_iota(jnp.int32, (8, LANES), 0)
    ).astype(BF16)
    for q in range(groups):
        tile = recv_v[8 * q]
        for n in range(1, 8):
            tile = tile + recv_v[8 * q + n]
        hi, lo = split(tile.T)
        spread = dot_nn(hi, expand) + dot_nn(lo, expand)
        spread = spread.reshape(8, 2, STK, LANES)
        for n in range(2):
            vexp[n, q * 8 * STK : (q + 1) * 8 * STK, :] = spread[:, n].reshape(8 * STK, LANES)

    def y_block(n):
        c, s = ey[n, 0], ey[n, 1]
        v_re, v_im = vexp[0], vexp[1]
        z = jnp.concatenate([v_re * c - v_im * s, v_re * s + v_im * c], axis=1)
        hi, lo = split(z)
        hot = onehot[...]
        return dot_nn(hot, hi) + dot_nn(hot, lo)

    def copy_y(k):
        off = band_offset(k)
        return copy_band(send_y.at[off], recv_y.at[b], y_ssem, y_rsem, off)

    def send_block(k):
        off = band_offset(k)
        send_y[off] = y_block((b + off) % nb)
        copy_y(k).start()

    loop(0, nb - 1, send_block)
    recv_y[b] = y_block(b)
    loop(0, nb - 1, lambda k: copy_y(k).wait_recv())

    field = recv_y[...].reshape(nb * 16, 2 * LANES).T
    f_re, f_im = field[:LANES], field[LANES:]
    left = jnp.concatenate(
        [jnp.concatenate([f_re, -f_im], axis=1), jnp.concatenate([f_im, f_re], axis=1)], axis=0
    )
    hi, lo = split(left)
    result = dot_nn(hi, tx[0]) + dot_nn(lo, tx[0]) + dot_nn(hi, tx[1])
    for n in range(2):
        for p in range(NPL):
            first = n * LANES + p * 16
            out_ref[n, p] = result[first : first + NXB, :nx]

    loop(0, steps, lambda s: copy_p(s).wait_send())
    loop(0, last, lambda i: copy_b(i).wait_send())
    loop(1, ng, lambda k: copy_ga(send_c, recv_c.at[j], c_ssem, c_rsem, k).wait_send())
    loop(1, ng, lambda k: copy_ga(send_a, recv_a.at[j], a_ssem, a_rsem, k).wait_send())
    loop(1, ng, lambda k: copy_v(k).wait_send())

    def end_band(k):
        off = band_offset(k)
        copy_band(send_z, recv_z.at[off], z_ssem, z_rsem, off).wait_send()
        copy_y(k).wait_send()

    loop(0, nb - 1, end_band)


def both_parts(table):
    hi = table.astype(jnp.bfloat16)
    lo = (table - hi.astype(np.float64)).astype(jnp.bfloat16)
    return np.stack([hi, lo])


def tables(nb, ng):
    nx, nz = NXB * nb, NPL * ng
    pad_z = round_up(nz, LANES)
    plane = np.arange(8 * ng) // 8 * NPL + np.arange(8 * ng) % 8
    angle = (plane[:, None] * np.arange(nz)[None, :] % nz) * (2 * np.pi / nz)
    real = (np.arange(8 * ng) % 8 < NPL)[:, None]
    tz = np.zeros((8 * ng, 2 * pad_z))
    tz[:, :nz] = np.where(real, np.cos(angle), 0.0)
    tz[:, pad_z : pad_z + nz] = np.where(real, np.sin(angle), 0.0)
    pad_x = round_up(nx, LANES)
    row = np.arange(16 * nb)
    x = row // 16 * NXB + row % 16
    angle = (x[:, None] * np.arange(nx)[None, :] % nx) * (2 * np.pi / nx)
    real = (row % 16 < NXB)[:, None]
    tx = np.zeros((2 * 16 * nb, pad_x))
    tx[: 16 * nb, :nx] = np.where(real, np.cos(angle), 0.0)
    tx[16 * nb :, :nx] = np.where(real, np.sin(angle), 0.0)
    first, second = np.triu_indices(NH)
    ell = np.array(ELL)
    parity = np.tile((ell[first] + ell[second]) % 2, SPECIES)
    even = np.zeros((2, KLANES), np.float32)
    even[0, : SPECIES * PAIRS] = 1 - parity
    even[1, : SPECIES * PAIRS] = -parity
    return jnp.asarray(both_parts(tz)), jnp.asarray(both_parts(tx)), jnp.asarray(even)


def on_device(
    waves, occupations, beta_table, wave_miller, atom_kinds, atom_sites, aug_table, stick_columns
):
    nb, ng = lax.axis_size("band"), lax.axis_size("ga")
    nx, nz = NXB * nb, NPL * ng
    atoms, slots = OWN_ATOMS * ng, STK * ng
    wave_count = waves.shape[2]
    gt_lanes = min(256, wave_count)
    tiles = wave_count // gt_lanes
    columns = STK * nz
    steps = ng // 2 // DESTS
    chips = ng // 2
    tz, tx, even = tables(nb, ng)
    vmem = pl.BlockSpec(memory_space=pltpu.VMEM)
    hbm = pl.BlockSpec(memory_space=pl.ANY)
    smem = pl.BlockSpec(memory_space=pltpu.SMEM)
    dma = pltpu.SemaphoreType.DMA
    return pl.pallas_call(
        functools.partial(kernel, nb, ng, gt_lanes),
        out_shape=jax.ShapeDtypeStruct((2, NPL, NXB, nx), F32),
        in_specs=[vmem, vmem, vmem, vmem, vmem, vmem, hbm, smem, hbm, hbm, vmem],
        out_specs=vmem,
        scratch_shapes=[
            pltpu.VMEM(aug_table.shape, BF16),
            pltpu.VMEM(tz.shape, BF16),
            pltpu.VMEM(tx.shape, BF16),
            dma((3,)),
            pltpu.VMEM((4, atoms, LANES), F32),
            pltpu.VMEM((8, wave_count), F32),
            pltpu.VMEM((tiles, 4 * gt_lanes, LANES), BF16),
            pltpu.VMEM((DESTS * ROWS, LANES), F32),
            pltpu.VMEM((steps, DESTS * ROWS, LANES), F32),
            pltpu.VMEM((steps, DESTS * ROWS, LANES), F32),
            pltpu.VMEM((chips, ROWS, LANES), F32),
            pltpu.VMEM((chips, ROWS, LANES), F32),
            pltpu.VMEM((STK, LANES), F32),
            pltpu.VMEM((ng, STK, LANES), F32),
            pltpu.VMEM((8, LANES), F32),
            pltpu.VMEM((2, atoms, columns), F32),
            pltpu.VMEM((OWN_ATOMS, 2 * LANES), F32),
            pltpu.VMEM((nb, OWN_ATOMS, 2 * LANES), F32),
            pltpu.VMEM((OWN_ATOMS, 2 * LANES), F32),
            pltpu.VMEM((ng, OWN_ATOMS, 2 * LANES), F32),
            pltpu.VMEM((atoms, KLANES), BF16),
            pltpu.VMEM((atoms, KLANES), BF16),
            pltpu.VMEM((8, round_up(columns, LANES)), F32),
            pltpu.VMEM((ng, 8, LANES), F32),
            pltpu.VMEM((ng, 8, LANES), F32),
            pltpu.VMEM((nb, 2, slots, LANES), F32),
            pltpu.VMEM((16, slots), BF16),
            pltpu.VMEM((2, slots, LANES), F32),
            pltpu.VMEM((nb, 16, 2 * LANES), F32),
            pltpu.VMEM((nb, 16, 2 * LANES), F32),
            dma((steps,)),
            dma((steps,)),
            dma((chips,)),
            dma((chips,)),
            dma((ng,)),
            dma((ng,)),
            dma((nb,)),
            dma((nb,)),
            dma((ng,)),
            dma((ng,)),
            dma((ng,)),
            dma((ng,)),
            dma((nb,)),
            dma((nb,)),
        ],
        compiler_params=pltpu.CompilerParams(
            collective_id=0, has_side_effects=True, vmem_limit_bytes=48 * 1024 * 1024
        ),
    )(
        waves,
        occupations[None],
        beta_table,
        wave_miller,
        atom_kinds[None],
        atom_sites,
        aug_table,
        stick_columns,
        tz,
        tx,
        even,
    )


def solution(mesh):
    in_specs = (
        P(None, "band", "ga"),
        P("band"),
        P(None, "ga"),
        P(None, "ga"),
        P(),
        P(),
        P(None, ("band", "ga")),
        P(("band", "ga")),
    )
    out_specs = P(None, "ga", "band", None)
    return jax.shard_map(
        on_device, mesh=mesh, in_specs=in_specs, out_specs=out_specs, check_vma=False
    )
```

profile of v0, /device:TPU:1, one launch (start us, length us, event | category | flops | bytes accessed | tf_op | source)
XLA Modules:
  0.0 87.6 jit_solution(1397109697617319096)
XLA Ops:
  0.0 0.0 copy-start
  0.0 1.7 %copy-done = bf16[684,1792]{1,0:T(8,128)(2,1)S(1)} copy-done((bf16[684,1792]{1,0:T(8,128)(2,1)S(1)}, bf16[684,1792]{1,0:T(8,128)(2,1)}, u32[]{:S(2)}) %copy-start) | copy-done | bytes 2451480
  1.7 0.0 copy-start.1
  1.7 1.0 %copy-done.1 = bf16[2,512,256]{2,1,0:T(8,128)(2,1)S(1)} copy-done((bf16[2,512,256]{2,1,0:T(8,128)(2,1)S(1)}, bf16[2,512,256]{2,1,0:T(8,128)(2,1)}, u32[]{:S(2)}) %copy-start.1) | copy-done | bytes 524312
  2.7 0.0 copy-start.2
  2.7 1.0 %copy-done.2 = bf16[2,256,512]{2,1,0:T(8,128)(2,1)S(1)} copy-done((bf16[2,256,512]{2,1,0:T(8,128)(2,1)S(1)}, bf16[2,256,512]{2,1,0:T(8,128)(2,1)}, u32[]{:S(2)}) %copy-start.2) | copy-done | bytes 524312
  3.8 0.0 copy-start.3
  3.8 1.0 %copy-done.3 = f32[72,1024]{1,0:T(8,128)S(1)} copy-done((f32[72,1024]{1,0:T(8,128)S(1)}, f32[72,1024]{1,0:T(8,128)}, u32[]{:S(2)}) %copy-start.3) | copy-done | bytes 294936
  4.7 0.0 copy-start.4
  4.7 0.9 %copy-done.4 = bf16[2,32,1024]{2,1,0:T(8,128)(2,1)S(1)} copy-done((bf16[2,32,1024]{2,1,0:T(8,128)(2,1)S(1)}, bf16[2,32,1024]{2,1,0:T(8,128)(2,1)}, u32[]{:S(2)}) %copy-start.4) | copy-done | bytes 131096
  5.6 0.0 copy-start.5
  5.7 0.7 copy-done.5
  6.4 0.0 copy-start.6
  6.4 0.7 copy-done.6
  7.1 0.0 copy-start.7
  7.1 0.7 copy-done.7
  7.7 0.0 copy-start.8
  7.7 0.7 copy-done.8
  8.4 0.0 copy-start.9
  8.4 0.7 copy-done.9
  9.1 0.0 copy-start.10
  9.1 0.7 copy-done.10
  9.7 77.0 %shard_map.109 = f32[2,7,15,240]{3,2,1,0:T(8,128)S(1)} custom-call(bf16[2,32,1024]{2,1,0:T(8,128)(2,1)S(1)} %copy-done.4, f32[1,32]{1,0:T(1,128)S(1)} %bitcast.3, f32[72,1024]{1,0:T(8,128)S(1)} %copy-done.3, s32[3,1024]{1,0:T(4,128)S(1)} %copy-done.5, s32[1,256]{1,0:T(1,128)S(1)} %bitcast.2, s32[3,256]{1,0:T(4,128)S(1)} %copy-done.7, ...), custom_call_target="tpu_custom_call" | custom-call | tf_op jit(solution)/shard_map/pallas_call | solution.py:587
  86.7 0.9 copy.12
Async XLA Ops:
  0.0 1.7 %copy-start = (bf16[684,1792]{1,0:T(8,128)(2,1)S(1)}, bf16[684,1792]{1,0:T(8,128)(2,1)}, u32[]{:S(2)}) copy-start(bf16[684,1792]{1,0:T(8,128)(2,1)} %tab_hbm.1) | copy-start | bytes 7354372
  1.7 1.0 %copy-start.1 = (bf16[2,512,256]{2,1,0:T(8,128)(2,1)S(1)}, bf16[2,512,256]{2,1,0:T(8,128)(2,1)}, u32[]{:S(2)}) copy-start(bf16[2,512,256]{2,1,0:T(8,128)(2,1)} %constant.7.clone.tx_hbm) | copy-start | bytes 1572868
  2.7 1.0 %copy-start.2 = (bf16[2,256,512]{2,1,0:T(8,128)(2,1)S(1)}, bf16[2,256,512]{2,1,0:T(8,128)(2,1)}, u32[]{:S(2)}) copy-start(bf16[2,256,512]{2,1,0:T(8,128)(2,1)} %constant.6.clone.tz_hbm) | copy-start | bytes 1572868
  3.8 1.0 %copy-start.3 = (f32[72,1024]{1,0:T(8,128)S(1)}, f32[72,1024]{1,0:T(8,128)}, u32[]{:S(2)}) copy-start(f32[72,1024]{1,0:T(8,128)} %beta_ref.1) | copy-start | bytes 884740
  4.7 0.9 %copy-start.4 = (bf16[2,32,1024]{2,1,0:T(8,128)(2,1)S(1)}, bf16[2,32,1024]{2,1,0:T(8,128)(2,1)}, u32[]{:S(2)}) copy-start(bf16[2,32,1024]{2,1,0:T(8,128)(2,1)} %waves_ref.1) | copy-start | bytes 393220
  5.6 0.7 copy-start.5
  6.4 0.7 copy-start.6
  7.1 0.7 copy-start.7
  7.7 0.7 copy-start.8
  8.4 0.7 copy-start.9
  9.1 0.7 copy-start.10
where the time goes:
time: 88 us; the launch traced here: 87.6 us
  Pallas kernels  77 us (88%)
  local copies, waits for them, and re-layouts  10.6 us (12%)
    pallas_call x1, Pallas kernels, on_device(): pl.pallas_call(functools.partial(kernel, nb, ng, gt_lanes), out_shape=jax...  77 us
    unnamed x22, local copies, waits for them, and re-layouts  9.72 us

commit v1 on v0

--- a/solution.py
+++ b/solution.py
@@ -20,6 +20,9 @@
 DESTS = 4
 LANES = 128
 KLANES = 768
+FOLD = OWN_ATOMS * 3 // 2
+VMEM_LIMIT = 67043328
+UNROLL = 4
 
 ELL = [0] * 2 + [1] * 6 + [2] * 10
 COS = (0.999999989, -19.7392045, 64.9391175, -85.4501395, 60.167631, -25.9675992, 6.52865816)
@@ -69,23 +72,33 @@
     nb,
     ng,
     gt_lanes,
+    waves_hbm,
+    occ_hbm,
+    beta_hbm,
+    mil_hbm,
+    kinds_hbm,
+    sites_hbm,
+    tab_hbm,
+    sticks_hbm,
+    tz_hbm,
+    tx_hbm,
+    even_hbm,
+    out_ref,
     waves_ref,
     occ_ref,
     beta_ref,
     mil_ref,
     kinds_ref,
     sites_ref,
-    tab_hbm,
     sticks_ref,
-    tz_hbm,
-    tx_hbm,
     even_ref,
-    out_ref,
     tab,
     tz,
     tx,
     local_sem,
     colb,
+    kindb,
+    species,
     mil,
     wmat,
     acc,
@@ -143,11 +156,20 @@
     chip_y = chip // cx
     chip_x = chip % cx
 
-    local = [
-        pltpu.make_async_copy(tab_hbm, tab, local_sem.at[0]),
-        pltpu.make_async_copy(tz_hbm, tz, local_sem.at[1]),
-        pltpu.make_async_copy(tx_hbm, tx, local_sem.at[2]),
+    ends = [
+        (sites_hbm, sites_ref),
+        (kinds_hbm, kinds_ref),
+        (mil_hbm, mil_ref),
+        (sticks_hbm, sticks_ref),
+        (waves_hbm, waves_ref),
+        (beta_hbm, beta_ref),
+        (occ_hbm, occ_ref),
+        (even_hbm, even_ref),
+        (tz_hbm, tz),
+        (tx_hbm, tx),
+        (tab_hbm, tab),
     ]
+    local = [pltpu.make_async_copy(*pair, local_sem.at[n]) for n, pair in enumerate(ends)]
     for copy in local:
         copy.start()
 
@@ -163,6 +185,9 @@
 
     lax.fori_loop(1, nb, greet_band, 0)
     lax.fori_loop(1, ng, greet_ga, 0)
+
+    for copy in local[:7]:
+        copy.wait()
 
     cols = jnp.concatenate(
         [
@@ -174,6 +199,15 @@
     ).T
     for n in range(4):
         colb[n] = jnp.broadcast_to(cols[:, n : n + 1], (atoms, LANES))
+    kindb[...] = colb[3].astype(jnp.int32)
+    kind_row = lax.broadcasted_iota(jnp.int32, (8, wave_count), 0)
+    for i in range(NH):
+        beta = [beta_ref[n * NH + i : n * NH + i + 1, :] for n in range(SPECIES)]
+        species[i] = jnp.where(
+            kind_row < 2,
+            jnp.where(kind_row < 1, beta[0], beta[1]),
+            jnp.where(kind_row < 3, beta[2], beta[3]),
+        )
     mil[0:3, :] = mil_ref[...].astype(F32)
     occ_row[...] = jnp.zeros(occ_row.shape, F32)
     occ_row[0:1, 0:band_dev] = occ_ref[...]
@@ -206,38 +240,51 @@
         return ((chip_y + e // cx) % cy) * cx + (chip_x + e % cx) % cx
 
     def project(step, parity):
-        acc[...] = jnp.zeros(acc.shape, F32)
-
-        def tile(g, carry):
-            lanes = pl.ds(pl.multiple_of(g * gt_lanes, gt_lanes), gt_lanes)
-            m1, m2, m3 = mil[0:1, lanes], mil[1:2, lanes], mil[2:3, lanes]
-            parts = [[], [], [], []]
-            for d in range(DESTS):
-                dest = 2 * chip_of(step * DESTS + d) + parity
-                rows = pl.ds(pl.multiple_of(dest * OWN_ATOMS, OWN_ATOMS), OWN_ATOMS)
-                p1, p2, p3, kind = (wide(colb[n, rows, :], gt_lanes) for n in range(4))
-                turns = turns_of(p1 * m1 + p2 * m2, nx) + turns_of(p3 * m3, nz)
-                c, s = cos_sin(turns)
-                pair = ((c, s), (-s, c), (-c, -s))
-                upper = kind > 1.5
-                odd_low = kind > 0.5
-                odd_high = kind > 2.5
+        def rows_of(d):
+            dest = 2 * chip_of(step * DESTS + d) + parity
+            return pl.ds(pl.multiple_of(dest * OWN_ATOMS, OWN_ATOMS), OWN_ATOMS)
+
+        def tile(g):
+            whole = [[], [], [], []]
+            for piece in range(gt_lanes // LANES):
+                lanes = pl.ds(pl.multiple_of(g * gt_lanes + piece * LANES, LANES), LANES)
+                m1, m2, m3 = mil[0:1, lanes], mil[1:2, lanes], mil[2:3, lanes]
+                pairs, kinds = [], []
+                for d in range(DESTS):
+                    rows = rows_of(d)
+                    p1, p2, p3 = (colb[n, rows, :] for n in range(3))
+                    kinds.append(kindb[rows, :])
+                    turns = turns_of(p1 * m1 + p2 * m2, nx) + turns_of(p3 * m3, nz)
+                    c, s = cos_sin(turns)
+                    pairs.append(((c, s), (-s, c), (-c, -s)))
+                parts = [[[None] * HALF for d in range(DESTS)] for n in range(4)]
                 for i in range(NH):
-                    beta = [beta_ref[n * NH + i : n * NH + i + 1, lanes] for n in range(SPECIES)]
-                    radial = jnp.where(
-                        upper,
-                        jnp.where(odd_high, beta[3], beta[2]),
-                        jnp.where(odd_low, beta[1], beta[0]),
-                    )
-                    first, second = pair[ELL[i]]
-                    h = i // HALF
-                    parts[2 * h].append(radial * first)
-                    parts[2 * h + 1].append(radial * second)
-            left = jnp.concatenate([jnp.concatenate(p, axis=0).astype(BF16) for p in parts], axis=1)
-            acc[...] += dot_nn(left, wmat[g])
+                    beta = species[i, :, lanes]
+                    for d in range(DESTS):
+                        radial = jnp.take_along_axis(beta, kinds[d], axis=0)
+                        first, second = pairs[d][ELL[i]]
+                        h = i // HALF
+                        parts[2 * h][d][i % HALF] = radial * first
+                        parts[2 * h + 1][d][i % HALF] = radial * second
+                for n in range(4):
+                    whole[n].append(jnp.concatenate(sum(parts[n], []), axis=0).astype(BF16))
+            left = jnp.concatenate(sum(whole, []), axis=1)
+            return dot_nn(left, wmat[g])
+
+        together = min(UNROLL, tiles)
+
+        def some(n, carry):
+            total = tile(n * together)
+            for g in range(1, together):
+                total = total + tile(n * together + g)
+            acc[...] = total if together == tiles else acc[...] + total
             return carry
 
-        lax.fori_loop(0, tiles, tile, 0)
+        if together == tiles:
+            some(0, 0)
+        else:
+            acc[...] = jnp.zeros(acc.shape, F32)
+            lax.fori_loop(0, tiles // together, some, 0)
 
     def for_partner(step, carry):
         project(step, 1 - core)
@@ -320,30 +367,24 @@
 
     lax.fori_loop(0, steps, for_owners, 0)
 
-    def phases(t):
-        lanes = pl.ds(pl.multiple_of(t * ct, ct), ct)
-        g = (lax.broadcasted_iota(jnp.int32, (1, ct), 1) + t * ct).astype(F32)
-        slot = jnp.floor((g + 0.5) * (1.0 / nz))
-        z = g - slot * nz
-        column = jnp.zeros((1, ct), F32)
-        for n in range(STK):
-            column = jnp.where(slot == n, stick[n], column)
-        x = jnp.floor((column + 0.5) * (1.0 / nx))
-        y = column - x * nx
-        x = x + (b * NXB).astype(F32)
-
-        def row(r):
-            rows = pl.ds(pl.multiple_of(r * 8, 8), 8)
-            p1, p2, p3 = (wide(colb[n, rows, :], ct) for n in range(3))
-            turns = turns_of(p1 * x + p2 * y, nx) + turns_of(p3 * z, nz)
-            c, s = cos_sin(turns)
-            phase[0, rows, lanes] = c
-            phase[1, rows, lanes] = s
-
-        loop(0, atoms // 8, row)
-
-    loop(0, NPL, phases)
-
+    loop(1, ng, lambda k: copy_ga(send_c, recv_c.at[j], c_ssem, c_rsem, k).wait_recv())
+    column = recv_c[...].reshape(slots, LANES)
+    slot_x = jnp.floor((column + 0.5) * (1.0 / nx))
+    slot_y = column - slot_x * nx
+    hot = (slot_x == lax.broadcasted_iota(jnp.int32, (slots, LANES), 1).astype(F32)).astype(F32)
+    onehot[...] = hot.T[0:16].astype(BF16)
+    lane_y = (lax.broadcasted_iota(jnp.int32, (1, LANES), 1) % 16).astype(F32)
+
+    def y_phases(n):
+        turns = turns_of(slot_y * (lane_y + (n * NXB).astype(F32)), nx)
+        c, s = cos_sin(turns)
+        ey[n, 0] = c
+        ey[n, 1] = s
+
+    loop(0, nb, y_phases)
+
+    loop(0, steps, lambda s: copy_p(s).wait_send())
+    loop(1, ng, lambda k: copy_ga(send_c, recv_c.at[j], c_ssem, c_rsem, k).wait_send())
     def wait_b(index):
         copy_b(index).wait_recv()
 
@@ -374,6 +415,8 @@
         piece = jnp.concatenate([piece, jnp.zeros((OWN_ATOMS, LANES), F32)], axis=1)
         shift = i * NH - i * (i - 1) // 2 - i
         total = total + (pltpu.roll(piece, shift, 1) if shift else piece)
+    folded = total[:4, LANES:] + pltpu.roll(total[4:, LANES:], LANES // 2, 1)
+    total = jnp.concatenate([total[:, :LANES], folded], axis=0)
     send_z[...] = total
     recv_z[0] = total
 
@@ -383,22 +426,33 @@
 
     loop(0, nb - 1, send_band)
 
-    loop(1, ng, lambda k: copy_ga(send_c, recv_c.at[j], c_ssem, c_rsem, k).wait_recv())
-    column = recv_c[...].reshape(slots, LANES)
-    slot_x = jnp.floor((column + 0.5) * (1.0 / nx))
-    slot_y = column - slot_x * nx
-    hot = (slot_x == lax.broadcasted_iota(jnp.int32, (slots, LANES), 1).astype(F32)).astype(F32)
-    onehot[...] = hot.T[0:16].astype(BF16)
-    lane_y = (lax.broadcasted_iota(jnp.int32, (1, LANES), 1) % 16).astype(F32)
-
-    def y_phases(n):
-        turns = turns_of(slot_y * (lane_y + (n * NXB).astype(F32)), nx)
-        c, s = cos_sin(turns)
-        ey[n, 0] = c
-        ey[n, 1] = s
-
-    loop(0, nb, y_phases)
-
+    def phases(t):
+        lanes = pl.ds(pl.multiple_of(t * ct, ct), ct)
+        g = (lax.broadcasted_iota(jnp.int32, (1, ct), 1) + t * ct).astype(F32)
+        slot = jnp.floor((g + 0.5) * (1.0 / nz))
+        z = g - slot * nz
+        column = jnp.zeros((1, ct), F32)
+        for n in range(STK):
+            column = jnp.where(slot == n, stick[n], column)
+        x = jnp.floor((column + 0.5) * (1.0 / nx))
+        y = column - x * nx
+        x = x + (b * NXB).astype(F32)
+
+        def row(r):
+            source = 2 * chip_of(last - r // 2) + r % 2
+            atom = pl.ds(pl.multiple_of(source * 8, 8), 8)
+            p1, p2, p3 = (wide(colb[n, atom, :], ct) for n in range(3))
+            rows = pl.ds(pl.multiple_of(r * 8, 8), 8)
+            turns = turns_of(p1 * x + p2 * y, nx) + turns_of(p3 * z, nz)
+            c, s = cos_sin(turns)
+            phase[0, rows, lanes] = c
+            phase[1, rows, lanes] = s
+
+        loop(0, atoms // 8, row)
+
+    loop(0, NPL, phases)
+
+    loop(0, last, lambda i: copy_b(i).wait_send())
     def wait_band(k):
         off = band_offset(k)
         copy_band(send_z, recv_z.at[off], z_ssem, z_rsem, off).wait_recv()
@@ -410,18 +464,44 @@
     send_a[...] = total
     recv_a[j] = total
     loop(1, ng, lambda k: copy_ga(send_a, recv_a.at[j], a_ssem, a_rsem, k).start())
-    for copy in local:
+    for copy in local[7:]:
         copy.wait()
-    loop(1, ng, lambda k: copy_ga(send_a, recv_a.at[j], a_ssem, a_rsem, k).wait_recv())
 
     even = even_ref[0:1, :]
     odd = even_ref[1:2, :]
-
-    def weights(r):
-        values = recv_a[pl.ds(2 * r, 2)].reshape(16, 2 * LANES)
+    depth = SPECIES * PAIRS
+    chips = cy * cx
+    part = chips // 2
+    augrow[...] = jnp.zeros(augrow.shape, F32)
+
+    def arrive(k):
+        copy_ga(send_a, recv_a.at[j], a_ssem, a_rsem, k).wait_recv()
+
+    def weights(index):
+        q = chip_of(last - index)
+
+        @pl.when(index == 0)
+        def _():
+            arrive((j - (chip * 2 + 1 - core)) % ng)
+
+        @pl.when(index > 0)
+        def _():
+            arrive((j - 2 * q) % ng)
+            arrive((j - 2 * q - 1) % ng)
+
+        values = []
+        for n in range(2):
+            got = recv_a[2 * q + n]
+            first, rest = got[:OWN_ATOMS], got[OWN_ATOMS:]
+            rest = jnp.concatenate([rest, pltpu.roll(rest, LANES // 2, 1)], axis=0)
+            values.append(jnp.concatenate([first, rest], axis=1))
+        values = jnp.concatenate(values, axis=0)
+        position = lax.broadcasted_iota(jnp.int32, values.shape, 1)
+        values = jnp.where(position < PAIRS, values, 0.0)
         values = jnp.concatenate([values, jnp.zeros((16, KLANES - 2 * LANES), F32)], axis=1)
-        rows = pl.ds(pl.multiple_of(r * 16, 16), 16)
-        kind = wide(colb[3, rows, :], KLANES)
+        atom = pl.ds(pl.multiple_of(q * 16, 16), 16)
+        rows = pl.ds(pl.multiple_of(index * 16, 16), 16)
+        kind = wide(colb[3, atom, :], KLANES)
         placed = jnp.where(kind < 0.5, values, 0.0)
         for n in range(1, SPECIES):
             moved = pltpu.roll(values, n * PAIRS, 1)
@@ -429,19 +509,19 @@
         wre[rows, :] = (placed * even).astype(BF16)
         wim[rows, :] = (placed * odd).astype(BF16)
 
-    loop(0, atoms // 16, weights)
-    depth = SPECIES * PAIRS
-
-    def coefficients(t):
-        lanes = pl.ds(pl.multiple_of(t * ct, ct), ct)
-        table = tab[:, lanes]
-        amp_re = dot_nn(wre[:, :depth], table)
-        amp_im = dot_nn(wim[:, :depth], table)
-        c, s = phase[0, :, lanes], phase[1, :, lanes]
-        augrow[0:1, lanes] = jnp.sum(amp_re * c + amp_im * s, axis=0, keepdims=True)
-        augrow[1:2, lanes] = jnp.sum(amp_im * c - amp_re * s, axis=0, keepdims=True)
-
-    loop(0, NPL, coefficients)
+    def half(h):
+        loop(part * h, part * (h + 1), weights)
+        rows = pl.ds(pl.multiple_of(h * part * 16, part * 16), part * 16)
+        for t in range(NPL):
+            lanes = slice(t * ct, (t + 1) * ct)
+            table = tab[:, lanes]
+            amp_re = dot_nn(wre[rows, :depth], table)
+            amp_im = dot_nn(wim[rows, :depth], table)
+            c, s = phase[0, rows, lanes], phase[1, rows, lanes]
+            augrow[0:1, lanes] += jnp.sum(amp_re * c + amp_im * s, axis=0, keepdims=True)
+            augrow[1:2, lanes] += jnp.sum(amp_im * c - amp_re * s, axis=0, keepdims=True)
+
+    loop(0, 2, half)
 
     pad_z = tz.shape[2] // 2
     wide_row = round_up(columns, LANES)
@@ -494,7 +574,7 @@
         z = jnp.concatenate([v_re * c - v_im * s, v_re * s + v_im * c], axis=1)
         hi, lo = split(z)
         hot = onehot[...]
-        return dot_nn(hot, hi) + dot_nn(hot, lo)
+        return (dot_nn(hot, hi) + dot_nn(hot, lo))[:NXB]
 
     def copy_y(k):
         off = band_offset(k)
@@ -507,9 +587,21 @@
 
     loop(0, nb - 1, send_block)
     recv_y[b] = y_block(b)
+
+    def end_band(k):
+        off = band_offset(k)
+        copy_band(send_z, recv_z.at[off], z_ssem, z_rsem, off).wait_send()
+
+    def end_ga(k):
+        copy_ga(send_a, recv_a.at[j], a_ssem, a_rsem, k).wait_send()
+        copy_v(k).wait_send()
+
+    loop(0, nb - 1, end_band)
+    loop(1, ng, end_ga)
     loop(0, nb - 1, lambda k: copy_y(k).wait_recv())
 
-    field = recv_y[...].reshape(nb * 16, 2 * LANES).T
+    gap = jnp.zeros((1, 2 * LANES), F32)
+    field = jnp.concatenate([x for n in range(nb) for x in (recv_y[n], gap)], axis=0).T
     f_re, f_im = field[:LANES], field[LANES:]
     left = jnp.concatenate(
         [jnp.concatenate([f_re, -f_im], axis=1), jnp.concatenate([f_im, f_re], axis=1)], axis=0
@@ -521,18 +613,7 @@
             first = n * LANES + p * 16
             out_ref[n, p] = result[first : first + NXB, :nx]
 
-    loop(0, steps, lambda s: copy_p(s).wait_send())
-    loop(0, last, lambda i: copy_b(i).wait_send())
-    loop(1, ng, lambda k: copy_ga(send_c, recv_c.at[j], c_ssem, c_rsem, k).wait_send())
-    loop(1, ng, lambda k: copy_ga(send_a, recv_a.at[j], a_ssem, a_rsem, k).wait_send())
-    loop(1, ng, lambda k: copy_v(k).wait_send())
-
-    def end_band(k):
-        off = band_offset(k)
-        copy_band(send_z, recv_z.at[off], z_ssem, z_rsem, off).wait_send()
-        copy_y(k).wait_send()
-
-    loop(0, nb - 1, end_band)
+    loop(0, nb - 1, lambda k: copy_y(k).wait_send())
 
 
 def both_parts(table):
@@ -581,20 +662,29 @@
     chips = ng // 2
     tz, tx, even = tables(nb, ng)
     vmem = pl.BlockSpec(memory_space=pltpu.VMEM)
-    hbm = pl.BlockSpec(memory_space=pl.ANY)
-    smem = pl.BlockSpec(memory_space=pltpu.SMEM)
+    hbm = pl.BlockSpec(memory_space=pltpu.HBM)
     dma = pltpu.SemaphoreType.DMA
     return pl.pallas_call(
         functools.partial(kernel, nb, ng, gt_lanes),
         out_shape=jax.ShapeDtypeStruct((2, NPL, NXB, nx), F32),
-        in_specs=[vmem, vmem, vmem, vmem, vmem, vmem, hbm, smem, hbm, hbm, vmem],
+        in_specs=[hbm] * 11,
         out_specs=vmem,
         scratch_shapes=[
+            pltpu.VMEM(waves.shape, BF16),
+            pltpu.VMEM((1, waves.shape[1]), F32),
+            pltpu.VMEM(beta_table.shape, F32),
+            pltpu.VMEM(wave_miller.shape, jnp.int32),
+            pltpu.VMEM((1, atoms), jnp.int32),
+            pltpu.VMEM(atom_sites.shape, jnp.int32),
+            pltpu.SMEM(stick_columns.shape, jnp.int32),
+            pltpu.VMEM(even.shape, F32),
             pltpu.VMEM(aug_table.shape, BF16),
             pltpu.VMEM(tz.shape, BF16),
             pltpu.VMEM(tx.shape, BF16),
-            dma((3,)),
+            dma((11,)),
             pltpu.VMEM((4, atoms, LANES), F32),
+            pltpu.VMEM((atoms, LANES), jnp.int32),
+            pltpu.VMEM((NH, 8, wave_count), F32),
             pltpu.VMEM((8, wave_count), F32),
             pltpu.VMEM((tiles, 4 * gt_lanes, LANES), BF16),
             pltpu.VMEM((DESTS * ROWS, LANES), F32),
@@ -606,10 +696,10 @@
             pltpu.VMEM((ng, STK, LANES), F32),
             pltpu.VMEM((8, LANES), F32),
             pltpu.VMEM((2, atoms, columns), F32),
-            pltpu.VMEM((OWN_ATOMS, 2 * LANES), F32),
-            pltpu.VMEM((nb, OWN_ATOMS, 2 * LANES), F32),
-            pltpu.VMEM((OWN_ATOMS, 2 * LANES), F32),
-            pltpu.VMEM((ng, OWN_ATOMS, 2 * LANES), F32),
+            pltpu.VMEM((FOLD, LANES), F32),
+            pltpu.VMEM((nb, FOLD, LANES), F32),
+            pltpu.VMEM((FOLD, LANES), F32),
+            pltpu.VMEM((ng, FOLD, LANES), F32),
             pltpu.VMEM((atoms, KLANES), BF16),
             pltpu.VMEM((atoms, KLANES), BF16),
             pltpu.VMEM((8, round_up(columns, LANES)), F32),
@@ -618,8 +708,8 @@
             pltpu.VMEM((nb, 2, slots, LANES), F32),
             pltpu.VMEM((16, slots), BF16),
             pltpu.VMEM((2, slots, LANES), F32),
-            pltpu.VMEM((nb, 16, 2 * LANES), F32),
-            pltpu.VMEM((nb, 16, 2 * LANES), F32),
+            pltpu.VMEM((nb, NXB, 2 * LANES), F32),
+            pltpu.VMEM((nb, NXB, 2 * LANES), F32),
             dma((steps,)),
             dma((steps,)),
             dma((chips,)),
@@ -636,7 +726,7 @@
             dma((nb,)),
         ],
         compiler_params=pltpu.CompilerParams(
-            collective_id=0, has_side_effects=True, vmem_limit_bytes=48 * 1024 * 1024
+            collective_id=0, has_side_effects=True, vmem_limit_bytes=VMEM_LIMIT
         ),
     )(
         waves,

time: 88 us -> 75.3 us (0.86)
  local copies, waits for them, and re-layouts: 10.6 us -> 1.79 us
  Pallas kernels: 77 us -> 73.3 us
    unnamed x22 -> x0, local copies, waits for them, and re-layouts: 9.72 us -> none
    pallas_call x1, Pallas kernels: 77 us -> 73.3 us  [on_device(): pl.pallas_call(functools.partial(kernel, nb, ng, gt_lanes), out_shape=jax...]
    pallas_call x1, local copies, waits for them, and re-layouts: 0.85 us -> 1.79 us  [on_device(): pl.pallas_call(functools.partial(kernel, nb, ng, gt_lanes), out_shape=jax...]
where the time goes in v1:
time: 75.3 us; the launch traced here: 75.1 us
  Pallas kernels  73.3 us (97%)
  local copies, waits for them, and re-layouts  1.79 us (2%)
    pallas_call x1, Pallas kernels, on_device(): pl.pallas_call(functools.partial(kernel, nb, ng, gt_lanes), out_shape=jax...  73.3 us
    pallas_call x1, local copies, waits for them, and re-layouts, on_device(): pl.pallas_call(functools.partial(kernel, nb, ng, gt_lanes), out_shape=jax...  1.79 us

profile of v1, /device:TPU:1, one launch (start us, length us, event | category | flops | bytes accessed | tf_op | source)
XLA Modules:
  0.0 75.1 jit_solution(18039534162595952887)
XLA Ops:
  0.0 73.3 %shard_map.109 = f32[2,7,15,240]{3,2,1,0:T(8,128)} custom-call(bf16[2,32,1024]{2,1,0:T(8,128)(2,1)} %waves_hbm.1, f32[1,32]{1,0:T(1,128)} %bitcast.3, f32[72,1024]{1,0:T(8,128)} %beta_hbm.1, s32[3,1024]{1,0:T(4,128)} %mil_hbm.1, s32[1,256]{1,0:T(1,128)} %bitcast.2, s32[3,256]{1,0:T(4,128)} %sites_hbm.1, bf16[684,1792]{1,0:T(8,128)(2,1)} %tab_hbm.1, ...), custom_call_target="tpu_custom_call" | custom-call | tf_op jit(solution)/shard_map/pallas_call | solution.py:667
  73.3 1.8 %copy.12 = f32[2,7,15,240]{3,0,2,1:T(2,128)} copy(f32[2,7,15,240]{3,2,1,0:T(8,128)} %shard_map.109) | data formatting | bytes 403200 | tf_op jit(solution)/shard_map/pallas_call | solution.py:667

commit v2 on v1

--- a/solution.py
+++ b/solution.py
@@ -1,4 +1,5 @@
 import functools
+import math
 
 import jax
 import jax.numpy as jnp
@@ -28,6 +29,14 @@
 COS = (0.999999989, -19.7392045, 64.9391175, -85.4501395, 60.167631, -25.9675992, 6.52865816)
 SIN = (6.28318492, -41.3415892, 81.5999433, -76.6144725, 41.3428824, -12.4712435)
 
+FULL = (
+    ((0, 2), (1, 2), (2, 2), (3, 2), (2, 0), (2, 3), (0, 3), (3, 0))
+    + ((3, 1), (1, 1), (0, 0), (0, 1), (1, 0), (1, 3), (2, 1), (3, 3)),
+    {0: (0, 1), 1: (0, 3), 2: (0, 1), 3: (0, 3), 4: (1, 0), 5: (3, 0)},
+    {11: (0,), 12: (4,), 13: (1,), 14: (2,), 15: (3, 5)},
+)
+SMALL = (((1, 1), (1, 0), (0, 1), (0, 0)), {}, {})
+
 MESH = pl.DeviceIdType.MESH
 F32 = jnp.float32
 BF16 = jnp.bfloat16
@@ -83,6 +92,7 @@
     tz_hbm,
     tx_hbm,
     even_hbm,
+    spread_hbm,
     out_ref,
     waves_ref,
     occ_ref,
@@ -92,6 +102,7 @@
     sites_ref,
     sticks_ref,
     even_ref,
+    spread_ref,
     tab,
     tz,
     tx,
@@ -106,6 +117,7 @@
     recv_p,
     send_b,
     recv_b,
+    recv_r,
     send_c,
     recv_c,
     occ_row,
@@ -128,6 +140,7 @@
     p_rsem,
     b_ssem,
     b_rsem,
+    r_rsem,
     c_ssem,
     c_rsem,
     z_ssem,
@@ -165,6 +178,7 @@
         (beta_hbm, beta_ref),
         (occ_hbm, occ_ref),
         (even_hbm, even_ref),
+        (spread_hbm, spread_ref),
         (tz_hbm, tz),
         (tx_hbm, tx),
         (tab_hbm, tab),
@@ -212,10 +226,9 @@
     occ_row[...] = jnp.zeros(occ_row.shape, F32)
     occ_row[0:1, 0:band_dev] = occ_ref[...]
     stick = [sticks_ref[t].astype(F32) for t in range(STK)]
-    slot_row = lax.broadcasted_iota(jnp.int32, (STK, LANES), 0)
-    mine = jnp.zeros((STK, LANES), F32)
+    mine = jnp.zeros((1, LANES), F32)
     for t in range(STK):
-        mine = jnp.where(slot_row == t, stick[t], mine)
+        mine = jnp.where(lax.broadcasted_iota(jnp.int32, (1, LANES), 1) == t, stick[t], mine)
     send_c[...] = mine
     recv_c[j] = mine
 
@@ -235,13 +248,25 @@
     def wide(x, lanes):
         return jnp.concatenate([x] * (lanes // LANES), axis=1) if lanes > LANES else x[:, :lanes]
 
-    def chip_of(index):
-        e = cy * cx - 1 - index
-        return ((chip_y + e // cx) % cy) * cx + (chip_x + e % cx) % cx
+    order, relays, added = FULL if ng == 32 else SMALL
+    last = cy * cx - 1
+
+    def chip_at(dy, dx):
+        return ((chip_y + dy) % cy) * cx + (chip_x + dx) % cx
+
+    def near_chip(index):
+        return chip_at(index // cx, index % cx)
+
+    def ordered_chip(step, d):
+        power = 1 + 3 * step + 9 * (step * (step - 1) // 2) + 27 * (step * (step - 1) * (step - 2) // 6)
+        code = [sum(order[n * DESTS + d][axis] * 4**n for n in range(steps)) for axis in range(2)]
+        return chip_at(*(value // power % 4 for value in code))
 
     def project(step, parity):
+        places = [ordered_chip(step, d) for d in range(DESTS)]
+
         def rows_of(d):
-            dest = 2 * chip_of(step * DESTS + d) + parity
+            dest = 2 * places[d] + parity
             return pl.ds(pl.multiple_of(dest * OWN_ATOMS, OWN_ATOMS), OWN_ATOMS)
 
         def tile(g):
@@ -340,57 +365,76 @@
     loop(1, ng, lambda k: copy_ga(send_c, recv_c.at[j], c_ssem, c_rsem, k).start())
 
     def copy_b(index):
+        target = chip_at(*relays.get(index, order[index]))
+        landed, sem = (recv_r, r_rsem) if index in relays else (recv_b, b_rsem)
         return pltpu.make_async_remote_copy(
             send_b.at[index],
-            recv_b.at[index],
+            landed.at[index],
             b_ssem.at[index],
-            b_rsem.at[index],
-            device_id=(b, 2 * chip_of(index) + core),
+            sem.at[index],
+            device_id=(b, 2 * target + core),
             device_id_type=MESH,
         )
 
-    last = cy * cx - 1
+    sent = [n for n in range(len(order)) if order[n] != (0, 0)]
+    direct = [n for n in sent if n not in relays]
+    own = order.index((0, 0))
 
     def for_owners(step, carry):
         project(step, core)
         copy_p(step).wait_recv()
-        for d in range(DESTS):
-            index = step * DESTS + d
-            block = acc[d * ROWS : (d + 1) * ROWS, :] + recv_p[step, d * ROWS : (d + 1) * ROWS, :]
-            send_b[index] = block
-
-            @pl.when(index < last)
-            def _():
-                copy_b(index).start()
-
+
+        def deliver(now):
+            for d in range(DESTS):
+                index = now * DESTS + d
+                rows = slice(d * ROWS, (d + 1) * ROWS)
+                send_b[index] = acc[rows, :] + recv_p[now, rows, :]
+                if index != own and index not in added:
+                    copy_b(index).start()
+
+        for now in range(steps):
+            pl.when(step == now)(functools.partial(deliver, now))
         return carry
 
     lax.fori_loop(0, steps, for_owners, 0)
+    for index in added:
+        block = send_b[index]
+        for n in added[index]:
+            copy_b(n).wait_recv()
+            block = block + recv_r[n]
+        send_b[index] = block
+        copy_b(index).start()
 
     loop(1, ng, lambda k: copy_ga(send_c, recv_c.at[j], c_ssem, c_rsem, k).wait_recv())
-    column = recv_c[...].reshape(slots, LANES)
+    owners = recv_c[:, 0, :]
+    column = jnp.concatenate(
+        [jnp.broadcast_to(owners[:, n : n + 1], (ng, LANES)) for n in range(STK)], axis=0
+    )
     slot_x = jnp.floor((column + 0.5) * (1.0 / nx))
-    slot_y = column - slot_x * nx
     hot = (slot_x == lax.broadcasted_iota(jnp.int32, (slots, LANES), 1).astype(F32)).astype(F32)
     onehot[...] = hot.T[0:16].astype(BF16)
+    vexp[0] = column - slot_x * nx
     lane_y = (lax.broadcasted_iota(jnp.int32, (1, LANES), 1) % 16).astype(F32)
-
-    def y_phases(n):
-        turns = turns_of(slot_y * (lane_y + (n * NXB).astype(F32)), nx)
-        c, s = cos_sin(turns)
-        ey[n, 0] = c
-        ey[n, 1] = s
-
-    loop(0, nb, y_phases)
+    some_rows = 32
+
+    def y_phases(r):
+        rows = pl.ds(pl.multiple_of(r * some_rows, some_rows), some_rows)
+        slot_y = vexp[0, rows, :]
+        c, s = cos_sin(turns_of(slot_y * lane_y, nx))
+        dc, ds = cos_sin(turns_of(slot_y * float(NXB), nx))
+        for n in range(nb):
+            ey[n, 0, rows, :] = c
+            ey[n, 1, rows, :] = s
+            c, s = c * dc - s * ds, s * dc + c * ds
+
+    loop(0, slots // some_rows, y_phases)
 
     loop(0, steps, lambda s: copy_p(s).wait_send())
     loop(1, ng, lambda k: copy_ga(send_c, recv_c.at[j], c_ssem, c_rsem, k).wait_send())
-    def wait_b(index):
+    for index in direct:
         copy_b(index).wait_recv()
-
-    loop(0, last, wait_b)
-    becp = send_b[last]
-    for index in range(last):
+    becp = send_b[own]
+    for index in direct:
         becp = becp + recv_b[index]
     occ = occ_row[...]
     occ = sum((pltpu.roll(occ, n * band_dev, 1) for n in range(1, LANES // band_dev)), occ)[0:1]
@@ -426,33 +470,42 @@
 
     loop(0, nb - 1, send_band)
 
-    def phases(t):
-        lanes = pl.ds(pl.multiple_of(t * ct, ct), ct)
-        g = (lax.broadcasted_iota(jnp.int32, (1, ct), 1) + t * ct).astype(F32)
-        slot = jnp.floor((g + 0.5) * (1.0 / nz))
-        z = g - slot * nz
-        column = jnp.zeros((1, ct), F32)
-        for n in range(STK):
-            column = jnp.where(slot == n, stick[n], column)
-        x = jnp.floor((column + 0.5) * (1.0 / nx))
-        y = column - x * nx
-        x = x + (b * NXB).astype(F32)
-
-        def row(r):
-            source = 2 * chip_of(last - r // 2) + r % 2
-            atom = pl.ds(pl.multiple_of(source * 8, 8), 8)
-            p1, p2, p3 = (wide(colb[n, atom, :], ct) for n in range(3))
-            rows = pl.ds(pl.multiple_of(r * 8, 8), 8)
-            turns = turns_of(p1 * x + p2 * y, nx) + turns_of(p3 * z, nz)
-            c, s = cos_sin(turns)
-            phase[0, rows, lanes] = c
-            phase[1, rows, lanes] = s
-
-        loop(0, atoms // 8, row)
-
-    loop(0, NPL, phases)
-
-    loop(0, last, lambda i: copy_b(i).wait_send())
+    column = jnp.zeros((1, LANES), F32)
+    for n in range(STK):
+        column = jnp.where(lane == n, stick[n], column)
+    stick_x = jnp.floor((column + 0.5) * (1.0 / nx))
+    stick_y = column - stick_x * nx
+    stick_x = stick_x + (b * NXB).astype(F32)
+    lane_tiles = phase.shape[2] // LANES
+    period = min(nz // math.gcd(nz, LANES), lane_tiles)
+    heights = []
+    for q in range(period):
+        g = (lane + q * LANES).astype(F32)
+        heights.append(g - nz * jnp.floor((g + 0.5) * (1.0 / nz)))
+
+    def phases(r):
+        source = 2 * near_chip(r // 2) + r % 2
+        atom = pl.ds(pl.multiple_of(source * 8, 8), 8)
+        p1, p2, p3 = (colb[n, atom, :] for n in range(3))
+        rows = pl.ds(pl.multiple_of(r * 8, 8), 8)
+        flat = cos_sin(turns_of(p1 * stick_x + p2 * stick_y, nx))
+        flat = [[jnp.broadcast_to(x[:, n : n + 1], (8, LANES)) for n in range(STK)] for x in flat]
+        tall = [cos_sin(turns_of(p3 * z, nz)) for z in heights]
+        for t in range(lane_tiles):
+            low = t * LANES // nz
+            high = min(((t + 1) * LANES - 1) // nz, STK - 1)
+            c, s = (x[low] for x in flat)
+            for n in range(low + 1, high + 1):
+                before = lane < n * nz - t * LANES
+                c, s = jnp.where(before, c, flat[0][n]), jnp.where(before, s, flat[1][n])
+            cz, sz = tall[t % period]
+            lanes = slice(t * LANES, (t + 1) * LANES)
+            phase[0, rows, lanes] = c * cz - s * sz
+            phase[1, rows, lanes] = s * cz + c * sz
+
+    loop(0, atoms // 8, phases)
+    for index in sent:
+        copy_b(index).wait_send()
     def wait_band(k):
         off = band_offset(k)
         copy_band(send_z, recv_z.at[off], z_ssem, z_rsem, off).wait_recv()
@@ -470,15 +523,14 @@
     even = even_ref[0:1, :]
     odd = even_ref[1:2, :]
     depth = SPECIES * PAIRS
-    chips = cy * cx
-    part = chips // 2
+    part = (last + 1) // 2
     augrow[...] = jnp.zeros(augrow.shape, F32)
 
     def arrive(k):
         copy_ga(send_a, recv_a.at[j], a_ssem, a_rsem, k).wait_recv()
 
     def weights(index):
-        q = chip_of(last - index)
+        q = near_chip(index)
 
         @pl.when(index == 0)
         def _():
@@ -540,11 +592,13 @@
     pair = jnp.concatenate(
         [jnp.concatenate([a_re, -a_im], axis=1), jnp.concatenate([a_im, a_re], axis=1)], axis=0
     )
-    group = lax.broadcasted_iota(jnp.int32, (LANES, 1), 0) // (2 * STK)
-    placed = jnp.where(group == j % 8, jnp.concatenate([pair] * 8, axis=0), 0.0)
-    hi, lo = split(placed)
+    hi, lo = split(jnp.concatenate([pair, jnp.zeros((LANES - 2 * STK, 2 * pad_z), F32)], axis=0))
     planes = dot_nt(tz[0], hi) + dot_nt(tz[0], lo) + dot_nt(tz[1], hi)
-    send_v[...] = planes.reshape(ng, 8, LANES)
+    plane_id = lax.broadcasted_iota(jnp.int32, planes.shape, 0) % 8
+    line = jnp.where(plane_id == 0, planes, 0.0)
+    for p in range(1, NPL):
+        line = line + pltpu.roll(jnp.where(plane_id == p, planes, 0.0), p * 2 * STK, 1)
+    send_v[:, 0, :] = jnp.sum(line.reshape(ng, 8, LANES), axis=1)
     recv_v[j] = send_v[j]
 
     def copy_v(k):
@@ -553,20 +607,12 @@
     loop(1, ng, lambda k: copy_v(k).start())
     loop(1, ng, lambda k: copy_v(k).wait_recv())
 
-    groups = max(ng // 8, 1)
-    expand = (
-        lax.broadcasted_iota(jnp.int32, (8, LANES), 1) // 16
-        == lax.broadcasted_iota(jnp.int32, (8, LANES), 0)
-    ).astype(BF16)
-    for q in range(groups):
-        tile = recv_v[8 * q]
-        for n in range(1, 8):
-            tile = tile + recv_v[8 * q + n]
-        hi, lo = split(tile.T)
-        spread = dot_nn(hi, expand) + dot_nn(lo, expand)
-        spread = spread.reshape(8, 2, STK, LANES)
-        for n in range(2):
-            vexp[n, q * 8 * STK : (q + 1) * 8 * STK, :] = spread[:, n].reshape(8 * STK, LANES)
+    hi, lo = split(recv_v[:, 0, :])
+    spread = dot_nn(jnp.concatenate([hi, lo], axis=1), spread_ref[...])
+    for n in range(2):
+        for t in range(STK):
+            first = (n * STK + t) * LANES
+            vexp[n, t * ng : (t + 1) * ng, :] = spread[:, first : first + LANES]
 
     def y_block(n):
         c, s = ey[n, 0], ey[n, 1]
@@ -645,7 +691,16 @@
     even = np.zeros((2, KLANES), np.float32)
     even[0, : SPECIES * PAIRS] = 1 - parity
     even[1, : SPECIES * PAIRS] = -parity
-    return jnp.asarray(both_parts(tz)), jnp.asarray(both_parts(tx)), jnp.asarray(even)
+    lane = np.arange(2 * STK * LANES)
+    source = lane % LANES // 16 * 16 + lane // LANES
+    spread = (np.arange(LANES)[:, None] == source[None, :]) & (lane % LANES // 16 < NPL)[None, :]
+    spread = np.concatenate([spread, spread]).astype(jnp.bfloat16)
+    return (
+        jnp.asarray(both_parts(tz)),
+        jnp.asarray(both_parts(tx)),
+        jnp.asarray(even),
+        jnp.asarray(spread),
+    )
 
 
 def on_device(
@@ -660,14 +715,14 @@
     columns = STK * nz
     steps = ng // 2 // DESTS
     chips = ng // 2
-    tz, tx, even = tables(nb, ng)
+    tz, tx, even, spread = tables(nb, ng)
     vmem = pl.BlockSpec(memory_space=pltpu.VMEM)
     hbm = pl.BlockSpec(memory_space=pltpu.HBM)
     dma = pltpu.SemaphoreType.DMA
     return pl.pallas_call(
         functools.partial(kernel, nb, ng, gt_lanes),
         out_shape=jax.ShapeDtypeStruct((2, NPL, NXB, nx), F32),
-        in_specs=[hbm] * 11,
+        in_specs=[hbm] * 12,
         out_specs=vmem,
         scratch_shapes=[
             pltpu.VMEM(waves.shape, BF16),
@@ -678,10 +733,11 @@
             pltpu.VMEM(atom_sites.shape, jnp.int32),
             pltpu.SMEM(stick_columns.shape, jnp.int32),
             pltpu.VMEM(even.shape, F32),
+            pltpu.VMEM(spread.shape, BF16),
             pltpu.VMEM(aug_table.shape, BF16),
             pltpu.VMEM(tz.shape, BF16),
             pltpu.VMEM(tx.shape, BF16),
-            dma((11,)),
+            dma((12,)),
             pltpu.VMEM((4, atoms, LANES), F32),
             pltpu.VMEM((atoms, LANES), jnp.int32),
             pltpu.VMEM((NH, 8, wave_count), F32),
@@ -692,10 +748,11 @@
             pltpu.VMEM((steps, DESTS * ROWS, LANES), F32),
             pltpu.VMEM((chips, ROWS, LANES), F32),
             pltpu.VMEM((chips, ROWS, LANES), F32),
-            pltpu.VMEM((STK, LANES), F32),
-            pltpu.VMEM((ng, STK, LANES), F32),
+            pltpu.VMEM((6, ROWS, LANES), F32),
+            pltpu.VMEM((1, LANES), F32),
+            pltpu.VMEM((ng, 1, LANES), F32),
             pltpu.VMEM((8, LANES), F32),
-            pltpu.VMEM((2, atoms, columns), F32),
+            pltpu.VMEM((2, atoms, round_up(columns, LANES)), F32),
             pltpu.VMEM((FOLD, LANES), F32),
             pltpu.VMEM((nb, FOLD, LANES), F32),
             pltpu.VMEM((FOLD, LANES), F32),
@@ -703,8 +760,8 @@
             pltpu.VMEM((atoms, KLANES), BF16),
             pltpu.VMEM((atoms, KLANES), BF16),
             pltpu.VMEM((8, round_up(columns, LANES)), F32),
-            pltpu.VMEM((ng, 8, LANES), F32),
-            pltpu.VMEM((ng, 8, LANES), F32),
+            pltpu.VMEM((ng, 1, LANES), F32),
+            pltpu.VMEM((ng, 1, LANES), F32),
             pltpu.VMEM((nb, 2, slots, LANES), F32),
             pltpu.VMEM((16, slots), BF16),
             pltpu.VMEM((2, slots, LANES), F32),
@@ -714,6 +771,7 @@
             dma((steps,)),
             dma((chips,)),
             dma((chips,)),
+            dma((6,)),
             dma((ng,)),
             dma((ng,)),
             dma((nb,)),
@@ -740,6 +798,7 @@
         tz,
         tx,
         even,
+        spread,
     )
 
 

time: 75.3 us -> 70.1 us (0.931)
  Pallas kernels: 73.3 us -> 68.1 us
    pallas_call x1, Pallas kernels: 73.3 us -> 68.1 us  [on_device(): pl.pallas_call(functools.partial(kernel, nb, ng, gt_lanes), out_shape=jax...]
where the time goes in v2:
time: 70.1 us; the launch traced here: 69.9 us
  Pallas kernels  68.1 us (97%)
  local copies, waits for them, and re-layouts  1.79 us (3%)
    pallas_call x1, Pallas kernels, on_device(): pl.pallas_call(functools.partial(kernel, nb, ng, gt_lanes), out_shape=jax...  68.1 us
    pallas_call x1, local copies, waits for them, and re-layouts, on_device(): pl.pallas_call(functools.partial(kernel, nb, ng, gt_lanes), out_shape=jax...  1.79 us

profile of v2, /device:TPU:1, one launch (start us, length us, event | category | flops | bytes accessed | tf_op | source)
XLA Modules:
  0.0 69.9 jit_solution(1872994196369711526)
XLA Ops:
  0.0 68.1 %shard_map.118 = f32[2,7,15,240]{3,2,1,0:T(8,128)} custom-call(bf16[2,32,1024]{2,1,0:T(8,128)(2,1)} %waves_hbm.1, f32[1,32]{1,0:T(1,128)} %bitcast.3, f32[72,1024]{1,0:T(8,128)} %beta_hbm.1, s32[3,1024]{1,0:T(4,128)} %mil_hbm.1, s32[1,256]{1,0:T(1,128)} %bitcast.2, s32[3,256]{1,0:T(4,128)} %sites_hbm.1, bf16[684,1792]{1,0:T(8,128)(2,1)} %tab_hbm.1, ...), custom_call_target="tpu_custom_call" | custom-call | tf_op jit(solution)/shard_map/pallas_call | solution.py:722
  68.1 1.8 %copy.13 = f32[2,7,15,240]{3,0,2,1:T(2,128)} copy(f32[2,7,15,240]{3,2,1,0:T(8,128)} %shard_map.118) | data formatting | bytes 403200 | tf_op jit(solution)/shard_map/pallas_call | solution.py:722

commit v3 on v2

--- a/solution.py
+++ b/solution.py
@@ -92,7 +92,6 @@
     tz_hbm,
     tx_hbm,
     even_hbm,
-    spread_hbm,
     out_ref,
     waves_ref,
     occ_ref,
@@ -102,7 +101,6 @@
     sites_ref,
     sticks_ref,
     even_ref,
-    spread_ref,
     tab,
     tz,
     tx,
@@ -126,16 +124,16 @@
     recv_z,
     send_a,
     recv_a,
-    wre,
-    wim,
+    wmix,
     augrow,
     send_v,
     recv_v,
+    recv_y,
     ey,
     onehot,
-    vexp,
-    send_y,
-    recv_y,
+    send_k,
+    recv_k,
+    field,
     p_ssem,
     p_rsem,
     b_ssem,
@@ -151,6 +149,8 @@
     v_rsem,
     y_ssem,
     y_rsem,
+    k_ssem,
+    k_rsem,
 ):
     nx, nz = NXB * nb, NPL * ng
     atoms = OWN_ATOMS * ng
@@ -178,7 +178,6 @@
         (beta_hbm, beta_ref),
         (occ_hbm, occ_ref),
         (even_hbm, even_ref),
-        (spread_hbm, spread_ref),
         (tz_hbm, tz),
         (tx_hbm, tx),
         (tab_hbm, tab),
@@ -189,16 +188,10 @@
 
     barrier = pltpu.get_barrier_semaphore()
 
-    def greet_ga(k, carry):
-        pl.semaphore_signal(barrier, inc=1, device_id=(b, (j + k) % ng), device_id_type=MESH)
-        return carry
-
-    def greet_band(k, carry):
-        pl.semaphore_signal(barrier, inc=1, device_id=((b + k) % nb, j), device_id_type=MESH)
-        return carry
-
-    lax.fori_loop(1, nb, greet_band, 0)
-    lax.fori_loop(1, ng, greet_ga, 0)
+    for k in range(1, nb):
+        pl.semaphore_signal(barrier, inc=1, device_id=(lax.rem(b + k, nb), j), device_id_type=MESH)
+    for k in range(1, ng):
+        pl.semaphore_signal(barrier, inc=1, device_id=(b, lax.rem(j + k, ng)), device_id_type=MESH)
 
     for copy in local[:7]:
         copy.wait()
@@ -237,13 +230,18 @@
         lanes = slice(g * gt_lanes, (g + 1) * gt_lanes)
         wr = waves_ref[0, :, lanes].astype(F32)
         wi = waves_ref[1, :, lanes].astype(F32)
-        none = jnp.zeros((LANES - width, gt_lanes), F32)
-        with_cos = jnp.concatenate([wr, wi], axis=0)
-        with_sin = jnp.concatenate([-wi, wr], axis=0)
-        for h in range(2):
-            for n, part in enumerate((with_cos, with_sin)):
-                full = jnp.concatenate([part, none] if h == 0 else [none, part], axis=0)
-                wmat[g, (2 * h + n) * gt_lanes : (2 * h + n + 1) * gt_lanes, :] = full.T.astype(BF16)
+        full = jnp.concatenate([wr, wi, -wi, wr], axis=0).T
+        swapped = pltpu.roll(full, width, 1)
+        low = lax.broadcasted_iota(jnp.int32, full.shape, 1) < width
+        for n, part in enumerate(
+            (
+                jnp.where(low, full, 0.0),
+                jnp.where(low, swapped, 0.0),
+                jnp.where(low, 0.0, swapped),
+                jnp.where(low, 0.0, full),
+            )
+        ):
+            wmat[g, n * gt_lanes : (n + 1) * gt_lanes, :] = part.astype(BF16)
 
     def wide(x, lanes):
         return jnp.concatenate([x] * (lanes // LANES), axis=1) if lanes > LANES else x[:, :lanes]
@@ -406,29 +404,24 @@
         copy_b(index).start()
 
     loop(1, ng, lambda k: copy_ga(send_c, recv_c.at[j], c_ssem, c_rsem, k).wait_recv())
-    owners = recv_c[:, 0, :]
-    column = jnp.concatenate(
-        [jnp.broadcast_to(owners[:, n : n + 1], (ng, LANES)) for n in range(STK)], axis=0
-    )
-    slot_x = jnp.floor((column + 0.5) * (1.0 / nx))
-    hot = (slot_x == lax.broadcasted_iota(jnp.int32, (slots, LANES), 1).astype(F32)).astype(F32)
-    onehot[...] = hot.T[0:16].astype(BF16)
-    vexp[0] = column - slot_x * nx
-    lane_y = (lax.broadcasted_iota(jnp.int32, (1, LANES), 1) % 16).astype(F32)
-    some_rows = 32
-
-    def y_phases(r):
-        rows = pl.ds(pl.multiple_of(r * some_rows, some_rows), some_rows)
-        slot_y = vexp[0, rows, :]
-        c, s = cos_sin(turns_of(slot_y * lane_y, nx))
-        dc, ds = cos_sin(turns_of(slot_y * float(NXB), nx))
-        for n in range(nb):
-            ey[n, 0, rows, :] = c
-            ey[n, 1, rows, :] = s
-            c, s = c * dc - s * ds, s * dc + c * ds
-
-    loop(0, slots // some_rows, y_phases)
-
+    owners = jnp.concatenate([recv_c[:, 0, :], jnp.zeros((LANES - ng, LANES), F32)], axis=0).T
+    per_row = min(LANES // ng, STK)
+    key_rows = STK // per_row
+    keys = []
+    for r in range(key_rows):
+        row = owners[r * per_row : r * per_row + 1]
+        for n in range(1, per_row):
+            at = r * per_row + n
+            row = row + pltpu.roll(owners[at : at + 1], n * ng, 1)
+        keys.append(row)
+    send_k[...] = jnp.concatenate(keys, axis=0)
+    recv_k[b] = send_k[...]
+
+    def send_keys(k):
+        off = band_offset(k)
+        copy_band(send_k, recv_k.at[b], k_ssem, k_rsem, off).start()
+
+    loop(0, nb - 1, send_keys)
     loop(0, steps, lambda s: copy_p(s).wait_send())
     loop(1, ng, lambda k: copy_ga(send_c, recv_c.at[j], c_ssem, c_rsem, k).wait_send())
     for index in direct:
@@ -529,18 +522,27 @@
     def arrive(k):
         copy_ga(send_a, recv_a.at[j], a_ssem, a_rsem, k).wait_recv()
 
-    def weights(index):
+    crowd = min(4, part)
+
+    def weights(n):
+        for index in range(crowd):
+            index = index + n * crowd
+            q = near_chip(index)
+
+            @pl.when(index == 0)
+            def _():
+                arrive((j - (chip * 2 + 1 - core)) % ng)
+
+            @pl.when(index > 0)
+            def _():
+                arrive((j - 2 * q) % ng)
+                arrive((j - 2 * q - 1) % ng)
+
+        for index in range(crowd):
+            weigh(index + n * crowd)
+
+    def weigh(index):
         q = near_chip(index)
-
-        @pl.when(index == 0)
-        def _():
-            arrive((j - (chip * 2 + 1 - core)) % ng)
-
-        @pl.when(index > 0)
-        def _():
-            arrive((j - 2 * q) % ng)
-            arrive((j - 2 * q - 1) % ng)
-
         values = []
         for n in range(2):
             got = recv_a[2 * q + n]
@@ -552,23 +554,26 @@
         values = jnp.where(position < PAIRS, values, 0.0)
         values = jnp.concatenate([values, jnp.zeros((16, KLANES - 2 * LANES), F32)], axis=1)
         atom = pl.ds(pl.multiple_of(q * 16, 16), 16)
-        rows = pl.ds(pl.multiple_of(index * 16, 16), 16)
+        first_im = (index // part + 1) * (part * 16)
+        rows = pl.ds(pl.multiple_of(first_im - part * 16 + index * 16, 16), 16)
         kind = wide(colb[3, atom, :], KLANES)
         placed = jnp.where(kind < 0.5, values, 0.0)
         for n in range(1, SPECIES):
             moved = pltpu.roll(values, n * PAIRS, 1)
             placed = jnp.where((kind > n - 0.5) & (kind < n + 0.5), moved, placed)
-        wre[rows, :] = (placed * even).astype(BF16)
-        wim[rows, :] = (placed * odd).astype(BF16)
+        wmix[rows, :] = (placed * even).astype(BF16)
+        rows = pl.ds(pl.multiple_of(first_im + index * 16, 16), 16)
+        wmix[rows, :] = (placed * odd).astype(BF16)
 
     def half(h):
-        loop(part * h, part * (h + 1), weights)
+        loop(part // crowd * h, part // crowd * (h + 1), weights)
         rows = pl.ds(pl.multiple_of(h * part * 16, part * 16), part * 16)
+        both_rows = pl.ds(pl.multiple_of(h * part * 32, part * 32), part * 32)
         for t in range(NPL):
             lanes = slice(t * ct, (t + 1) * ct)
             table = tab[:, lanes]
-            amp_re = dot_nn(wre[rows, :depth], table)
-            amp_im = dot_nn(wim[rows, :depth], table)
+            amp = dot_nn(wmix[both_rows, :depth], table)
+            amp_re, amp_im = amp[: part * 16], amp[part * 16 :]
             c, s = phase[0, rows, lanes], phase[1, rows, lanes]
             augrow[0:1, lanes] += jnp.sum(amp_re * c + amp_im * s, axis=0, keepdims=True)
             augrow[1:2, lanes] += jnp.sum(amp_im * c - amp_re * s, axis=0, keepdims=True)
@@ -605,34 +610,6 @@
         return copy_ga(send_v.at[(j + k) % ng], recv_v.at[j], v_ssem, v_rsem, k)
 
     loop(1, ng, lambda k: copy_v(k).start())
-    loop(1, ng, lambda k: copy_v(k).wait_recv())
-
-    hi, lo = split(recv_v[:, 0, :])
-    spread = dot_nn(jnp.concatenate([hi, lo], axis=1), spread_ref[...])
-    for n in range(2):
-        for t in range(STK):
-            first = (n * STK + t) * LANES
-            vexp[n, t * ng : (t + 1) * ng, :] = spread[:, first : first + LANES]
-
-    def y_block(n):
-        c, s = ey[n, 0], ey[n, 1]
-        v_re, v_im = vexp[0], vexp[1]
-        z = jnp.concatenate([v_re * c - v_im * s, v_re * s + v_im * c], axis=1)
-        hi, lo = split(z)
-        hot = onehot[...]
-        return (dot_nn(hot, hi) + dot_nn(hot, lo))[:NXB]
-
-    def copy_y(k):
-        off = band_offset(k)
-        return copy_band(send_y.at[off], recv_y.at[b], y_ssem, y_rsem, off)
-
-    def send_block(k):
-        off = band_offset(k)
-        send_y[off] = y_block((b + off) % nb)
-        copy_y(k).start()
-
-    loop(0, nb - 1, send_block)
-    recv_y[b] = y_block(b)
 
     def end_band(k):
         off = band_offset(k)
@@ -642,13 +619,94 @@
         copy_ga(send_a, recv_a.at[j], a_ssem, a_rsem, k).wait_send()
         copy_v(k).wait_send()
 
+    def wait_keys(k):
+        off = band_offset(k)
+        copy_band(send_k, recv_k.at[b], k_ssem, k_rsem, off).wait_recv()
+        copy_band(send_k, recv_k.at[b], k_ssem, k_rsem, off).wait_send()
+
+    loop(0, nb - 1, wait_keys)
+    keys = jnp.concatenate([recv_k[n] for n in range(nb)], axis=0)
+    slot_x = jnp.floor((keys + 0.5) * (1.0 / nx))
+    slot_y = keys - slot_x * nx
+    spare = jnp.zeros((LANES - nb * key_rows, LANES), F32)
+    slot_y = jnp.concatenate([slot_y, spare], axis=0).T
+    row_x = lax.broadcasted_iota(jnp.int32, (16, LANES), 0).astype(F32)
+    held = per_row * ng
+    for n in range(nb):
+        for r in range(key_rows):
+            at = n * key_rows + r
+            hot = jnp.where(row_x == slot_x[at : at + 1], 1.0, 0.0).astype(BF16)
+            onehot[n, :, r * held : (r + 1) * held] = hot[:, :held]
+            onehot[n, :, slots + r * held : slots + (r + 1) * held] = hot[:, :held]
+            ey[n, 0, r * held : (r + 1) * held, :] = jnp.broadcast_to(
+                slot_y[:held, at : at + 1], (held, LANES)
+            )
+    lane_y = (lax.broadcasted_iota(jnp.int32, (1, LANES), 1) % 16).astype(F32) + (b * NXB).astype(F32)
+    some_rows = 64
+
+    def y_phases(r):
+        n = r // (slots // some_rows)
+        rows = pl.ds(pl.multiple_of(r % (slots // some_rows) * some_rows, some_rows), some_rows)
+        c, s = cos_sin(turns_of(ey[n, 0, rows, :] * lane_y, nx))
+        ey[n, 0, rows, :] = c
+        ey[n, 1, rows, :] = s
+
+    loop(0, nb * (slots // some_rows), y_phases)
     loop(0, nb - 1, end_band)
+    loop(1, ng, lambda k: copy_v(k).wait_recv())
+
+    if nb == 16:
+        hops = {n: (0, n) for n in (5, -5, 1, -1, 2, -2)}
+        hops.update({5 + n: (5, n) for n in (3, 2, -2, 1, -1)})
+        hops.update({-5 + n: (-5, n) for n in (2, -2, 1, -1)})
+    else:
+        hops = {n: (0, n) for n in range(1, nb)}
+
+    def copy_y(off):
+        back, hop = hops[off]
+        slot = recv_y.at[(b + nb - back) % nb]
+        return pltpu.make_async_remote_copy(
+            slot,
+            slot,
+            y_ssem.at[off % nb],
+            y_rsem.at[off % nb],
+            device_id=((b + nb + hop) % nb, j),
+            device_id_type=MESH,
+        )
+
+    def pass_on(back):
+        for off in hops:
+            if hops[off][0] == back:
+                copy_y(off).start()
+
+    recv_y[b] = recv_v[:, 0, :]
+    pass_on(0)
     loop(1, ng, end_ga)
-    loop(0, nb - 1, lambda k: copy_y(k).wait_recv())
-
-    gap = jnp.zeros((1, 2 * LANES), F32)
-    field = jnp.concatenate([x for n in range(nb) for x in (recv_y[n], gap)], axis=0).T
-    f_re, f_im = field[:LANES], field[LANES:]
+
+    group = lax.broadcasted_iota(jnp.int32, (2 * ng, LANES), 1) // 16 * 16
+
+    def take_blocks(sources):
+        values = jnp.concatenate([recv_y[source] for source in sources], axis=0)
+        pick = group[: len(sources) * ng]
+        picked = [jnp.take_along_axis(values, pick + n, axis=1) for n in range(2 * STK)]
+        for k, source in enumerate(sources):
+            own = [x[k * ng : (k + 1) * ng] for x in picked]
+            v_re, v_im = jnp.concatenate(own[:STK], axis=0), jnp.concatenate(own[STK:], axis=0)
+            c, s = ey[source, 0], ey[source, 1]
+            z = jnp.concatenate([v_re * c - v_im * s, v_re * s + v_im * c], axis=1)
+            rows = pl.ds(pl.multiple_of(source * 16, 16), 16)
+            field[rows, :] = dot_nn(onehot[source], jnp.concatenate(split(z), axis=0))
+
+    take_blocks([b])
+    groups_of = [(5, -5), (1, -1), (2, -2), (3, -3), (4, -4), (6, -6), (7, -7), (8,)]
+    for offs in groups_of if nb == 16 else [(n,) for n in range(1, nb)]:
+        for off in offs:
+            copy_y(off).wait_recv()
+            pass_on(off)
+        take_blocks([(b + nb - off) % nb for off in offs])
+
+    turned = field[...].T
+    f_re, f_im = turned[:LANES], turned[LANES:]
     left = jnp.concatenate(
         [jnp.concatenate([f_re, -f_im], axis=1), jnp.concatenate([f_im, f_re], axis=1)], axis=0
     )
@@ -659,7 +717,8 @@
             first = n * LANES + p * 16
             out_ref[n, p] = result[first : first + NXB, :nx]
 
-    loop(0, nb - 1, lambda k: copy_y(k).wait_send())
+    for off in hops:
+        copy_y(off).wait_send()
 
 
 def both_parts(table):
@@ -691,15 +750,10 @@
     even = np.zeros((2, KLANES), np.float32)
     even[0, : SPECIES * PAIRS] = 1 - parity
     even[1, : SPECIES * PAIRS] = -parity
-    lane = np.arange(2 * STK * LANES)
-    source = lane % LANES // 16 * 16 + lane // LANES
-    spread = (np.arange(LANES)[:, None] == source[None, :]) & (lane % LANES // 16 < NPL)[None, :]
-    spread = np.concatenate([spread, spread]).astype(jnp.bfloat16)
     return (
         jnp.asarray(both_parts(tz)),
         jnp.asarray(both_parts(tx)),
         jnp.asarray(even),
-        jnp.asarray(spread),
     )
 
 
@@ -715,14 +769,15 @@
     columns = STK * nz
     steps = ng // 2 // DESTS
     chips = ng // 2
-    tz, tx, even, spread = tables(nb, ng)
+    key_rows = STK // min(LANES // ng, STK)
+    tz, tx, even = tables(nb, ng)
     vmem = pl.BlockSpec(memory_space=pltpu.VMEM)
     hbm = pl.BlockSpec(memory_space=pltpu.HBM)
     dma = pltpu.SemaphoreType.DMA
     return pl.pallas_call(
         functools.partial(kernel, nb, ng, gt_lanes),
         out_shape=jax.ShapeDtypeStruct((2, NPL, NXB, nx), F32),
-        in_specs=[hbm] * 12,
+        in_specs=[hbm] * 11,
         out_specs=vmem,
         scratch_shapes=[
             pltpu.VMEM(waves.shape, BF16),
@@ -733,11 +788,10 @@
             pltpu.VMEM(atom_sites.shape, jnp.int32),
             pltpu.SMEM(stick_columns.shape, jnp.int32),
             pltpu.VMEM(even.shape, F32),
-            pltpu.VMEM(spread.shape, BF16),
             pltpu.VMEM(aug_table.shape, BF16),
             pltpu.VMEM(tz.shape, BF16),
             pltpu.VMEM(tx.shape, BF16),
-            dma((12,)),
+            dma((11,)),
             pltpu.VMEM((4, atoms, LANES), F32),
             pltpu.VMEM((atoms, LANES), jnp.int32),
             pltpu.VMEM((NH, 8, wave_count), F32),
@@ -757,16 +811,16 @@
             pltpu.VMEM((nb, FOLD, LANES), F32),
             pltpu.VMEM((FOLD, LANES), F32),
             pltpu.VMEM((ng, FOLD, LANES), F32),
-            pltpu.VMEM((atoms, KLANES), BF16),
-            pltpu.VMEM((atoms, KLANES), BF16),
+            pltpu.VMEM((2 * atoms, KLANES), BF16),
             pltpu.VMEM((8, round_up(columns, LANES)), F32),
             pltpu.VMEM((ng, 1, LANES), F32),
             pltpu.VMEM((ng, 1, LANES), F32),
+            pltpu.VMEM((nb, ng, LANES), F32),
             pltpu.VMEM((nb, 2, slots, LANES), F32),
-            pltpu.VMEM((16, slots), BF16),
-            pltpu.VMEM((2, slots, LANES), F32),
-            pltpu.VMEM((nb, NXB, 2 * LANES), F32),
-            pltpu.VMEM((nb, NXB, 2 * LANES), F32),
+            pltpu.VMEM((nb, 16, 2 * slots), BF16),
+            pltpu.VMEM((key_rows, LANES), F32),
+            pltpu.VMEM((nb, key_rows, LANES), F32),
+            pltpu.VMEM((nb * 16, 2 * LANES), F32),
             dma((steps,)),
             dma((steps,)),
             dma((chips,)),
@@ -780,6 +834,8 @@
             dma((ng,)),
             dma((ng,)),
             dma((ng,)),
+            dma((nb,)),
+            dma((nb,)),
             dma((nb,)),
             dma((nb,)),
         ],
@@ -798,7 +854,6 @@
         tz,
         tx,
         even,
-        spread,
     )
 
 

time: 70.1 us -> 67 us (0.956); the launches traced: 69.9 us -> 65.9 us
  Pallas kernels: 68.1 us -> 64.1 us
    pallas_call x1, Pallas kernels: 68.1 us -> 64.1 us  [on_device(): pl.pallas_call(functools.partial(kernel, nb, ng, gt_lanes), out_shape=jax...]
where the time goes in v3:
time: 67 us; the launch traced here: 65.9 us
  Pallas kernels  64.1 us (96%)
  local copies, waits for them, and re-layouts  1.79 us (3%)
    pallas_call x1, Pallas kernels, on_device(): pl.pallas_call(functools.partial(kernel, nb, ng, gt_lanes), out_shape=jax...  64.1 us
    pallas_call x1, local copies, waits for them, and re-layouts, on_device(): pl.pallas_call(functools.partial(kernel, nb, ng, gt_lanes), out_shape=jax...  1.79 us

profile of v3, /device:TPU:1, one launch (start us, length us, event | category | flops | bytes accessed | tf_op | source)
XLA Modules:
  0.0 65.9 jit_solution(7042400826519492289)
XLA Ops:
  0.0 64.1 %shard_map.109 = f32[2,7,15,240]{3,2,1,0:T(8,128)} custom-call(bf16[2,32,1024]{2,1,0:T(8,128)(2,1)} %waves_hbm.1, f32[1,32]{1,0:T(1,128)} %bitcast.3, f32[72,1024]{1,0:T(8,128)} %beta_hbm.1, s32[3,1024]{1,0:T(4,128)} %mil_hbm.1, s32[1,256]{1,0:T(1,128)} %bitcast.2, s32[3,256]{1,0:T(4,128)} %sites_hbm.1, bf16[684,1792]{1,0:T(8,128)(2,1)} %tab_hbm.1, ...), custom_call_target="tpu_custom_call" | custom-call | tf_op jit(solution)/shard_map/pallas_call | solution.py:777
  64.1 1.8 %copy.12 = f32[2,7,15,240]{3,0,2,1:T(2,128)} copy(f32[2,7,15,240]{3,2,1,0:T(8,128)} %shard_map.109) | data formatting | bytes 403200 | tf_op jit(solution)/shard_map/pallas_call | solution.py:777

commit v4 on v3

--- a/solution.py
+++ b/solution.py
@@ -40,7 +40,6 @@
 MESH = pl.DeviceIdType.MESH
 F32 = jnp.float32
 BF16 = jnp.bfloat16
-highest = lax.Precision.HIGHEST
 
 
 def round_up(value, step):
@@ -69,12 +68,12 @@
     return hi, (x - hi.astype(F32)).astype(BF16)
 
 
-def dot_nt(a, b, **kw):
-    return lax.dot_general(a, b, (((1,), (1,)), ((), ())), preferred_element_type=F32, **kw)
-
-
-def dot_nn(a, b, **kw):
-    return lax.dot_general(a, b, (((1,), (0,)), ((), ())), preferred_element_type=F32, **kw)
+def dot_nt(a, b):
+    return lax.dot_general(a, b, (((1,), (1,)), ((), ())), preferred_element_type=F32)
+
+
+def dot_nn(a, b):
+    return lax.dot_general(a, b, (((1,), (0,)), ((), ())), preferred_element_type=F32)
 
 
 def kernel(
@@ -333,7 +332,7 @@
             target,
             ssem.at[k],
             rsem.at[k],
-            device_id=(b, (j + k) % ng),
+            device_id=(b, lax.rem(j + k, ng)),
             device_id_type=MESH,
         )
 
@@ -360,7 +359,8 @@
         lax.fori_loop(low, high, step, 0)
 
     loop(0, steps, lambda s: copy_p(s).start())
-    loop(1, ng, lambda k: copy_ga(send_c, recv_c.at[j], c_ssem, c_rsem, k).start())
+    for k in range(1, ng):
+        copy_ga(send_c, recv_c.at[j], c_ssem, c_rsem, k).start()
 
     def copy_b(index):
         target = chip_at(*relays.get(index, order[index]))
@@ -434,7 +434,11 @@
     lane = lax.broadcasted_iota(jnp.int32, (1, LANES), 1)
     occ = jnp.where(lane < width, occ, 0.0)
     both = jnp.concatenate([becp, pltpu.roll(becp, LANES - width, 1)], axis=0)
-    gram = dot_nt(both * occ, both, precision=highest)
+    hi, lo = split(both)
+    occ_hi, occ_lo = split(both * occ)
+    gram = dot_nt(
+        jnp.concatenate([occ_hi, occ_hi, occ_lo], axis=1), jnp.concatenate([hi, lo, hi], axis=1)
+    )
     rows = NH * OWN_ATOMS
     row_id = lax.broadcasted_iota(jnp.int32, (rows, rows), 0)
     col_id = lax.broadcasted_iota(jnp.int32, (rows, rows), 1)
@@ -442,8 +446,8 @@
     pick = (
         lax.broadcasted_iota(jnp.int32, (rows, LANES), 0) // OWN_ATOMS
         == lax.broadcasted_iota(jnp.int32, (rows, LANES), 1)
-    ).astype(F32)
-    square = dot_nn(gram, pick, precision=highest)
+    ).astype(BF16)
+    square = dot_nn(jnp.concatenate(split(gram), axis=1), jnp.concatenate([pick, pick], axis=0))
     total = jnp.zeros((OWN_ATOMS, 2 * LANES), F32)
     for i in range(NH):
         factor = jnp.where(lane < i, 0.0, jnp.where(lane == i, 1.0, 2.0))
@@ -509,14 +513,15 @@
         total = total + recv_z[n]
     send_a[...] = total
     recv_a[j] = total
-    loop(1, ng, lambda k: copy_ga(send_a, recv_a.at[j], a_ssem, a_rsem, k).start())
+    for k in range(1, ng):
+        copy_ga(send_a, recv_a.at[j], a_ssem, a_rsem, k).start()
     for copy in local[7:]:
         copy.wait()
 
     even = even_ref[0:1, :]
     odd = even_ref[1:2, :]
     depth = SPECIES * PAIRS
-    part = (last + 1) // 2
+    part = last + 1
     augrow[...] = jnp.zeros(augrow.shape, F32)
 
     def arrive(k):
@@ -578,7 +583,7 @@
             augrow[0:1, lanes] += jnp.sum(amp_re * c + amp_im * s, axis=0, keepdims=True)
             augrow[1:2, lanes] += jnp.sum(amp_im * c - amp_re * s, axis=0, keepdims=True)
 
-    loop(0, 2, half)
+    loop(0, (last + 1) // part, half)
 
     pad_z = tz.shape[2] // 2
     wide_row = round_up(columns, LANES)
@@ -607,9 +612,10 @@
     recv_v[j] = send_v[j]
 
     def copy_v(k):
-        return copy_ga(send_v.at[(j + k) % ng], recv_v.at[j], v_ssem, v_rsem, k)
-
-    loop(1, ng, lambda k: copy_v(k).start())
+        return copy_ga(send_v.at[lax.rem(j + k, ng)], recv_v.at[j], v_ssem, v_rsem, k)
+
+    for k in range(1, ng):
+        copy_v(k).start()
 
     def end_band(k):
         off = band_offset(k)
@@ -698,12 +704,13 @@
             field[rows, :] = dot_nn(onehot[source], jnp.concatenate(split(z), axis=0))
 
     take_blocks([b])
-    groups_of = [(5, -5), (1, -1), (2, -2), (3, -3), (4, -4), (6, -6), (7, -7), (8,)]
+    groups_of = [(5, -5), (1, -1, 2, -2), (3, -3, 4, -4, 6, -6, 7, -7, 8)]
     for offs in groups_of if nb == 16 else [(n,) for n in range(1, nb)]:
         for off in offs:
             copy_y(off).wait_recv()
             pass_on(off)
-        take_blocks([(b + nb - off) % nb for off in offs])
+        for n in range(0, len(offs), 2):
+            take_blocks([(b + nb - off) % nb for off in offs[n : n + 2]])
 
     turned = field[...].T
     f_re, f_im = turned[:LANES], turned[LANES:]
@@ -711,7 +718,8 @@
         [jnp.concatenate([f_re, -f_im], axis=1), jnp.concatenate([f_im, f_re], axis=1)], axis=0
     )
     hi, lo = split(left)
-    result = dot_nn(hi, tx[0]) + dot_nn(lo, tx[0]) + dot_nn(hi, tx[1])
+    result = dot_nn(jnp.concatenate([hi, lo], axis=0), tx[0])
+    result = result[: 2 * LANES] + result[2 * LANES :] + dot_nn(hi, tx[1])
     for n in range(2):
         for p in range(NPL):
             first = n * LANES + p * 16

time: 67 us -> 66.9 us (level); the launches traced: 65.9 us -> 66.7 us
  Pallas kernels: 64.1 us -> 64.9 us
    pallas_call x1, Pallas kernels: 64.1 us -> 64.9 us  [on_device(): pl.pallas_call(functools.partial(kernel, nb, ng, gt_lanes), out_shape=jax...]
where the time goes in v4:
time: 66.9 us; the launch traced here: 66.7 us
  Pallas kernels  64.9 us (97%)
  local copies, waits for them, and re-layouts  1.79 us (3%)
    pallas_call x1, Pallas kernels, on_device(): pl.pallas_call(functools.partial(kernel, nb, ng, gt_lanes), out_shape=jax...  64.9 us
    pallas_call x1, local copies, waits for them, and re-layouts, on_device(): pl.pallas_call(functools.partial(kernel, nb, ng, gt_lanes), out_shape=jax...  1.79 us

profile of v4, /device:TPU:1, one launch (start us, length us, event | category | flops | bytes accessed | tf_op | source)
XLA Modules:
  0.0 66.7 jit_solution(15026054202757395366)
XLA Ops:
  0.0 64.9 %shard_map.109 = f32[2,7,15,240]{3,2,1,0:T(8,128)} custom-call(bf16[2,32,1024]{2,1,0:T(8,128)(2,1)} %waves_hbm.1, f32[1,32]{1,0:T(1,128)} %bitcast.3, f32[72,1024]{1,0:T(8,128)} %beta_hbm.1, s32[3,1024]{1,0:T(4,128)} %mil_hbm.1, s32[1,256]{1,0:T(1,128)} %bitcast.2, s32[3,256]{1,0:T(4,128)} %sites_hbm.1, bf16[684,1792]{1,0:T(8,128)(2,1)} %tab_hbm.1, ...), custom_call_target="tpu_custom_call" | custom-call | tf_op jit(solution)/shard_map/pallas_call | solution.py:785
  64.9 1.8 %copy.12 = f32[2,7,15,240]{3,0,2,1:T(2,128)} copy(f32[2,7,15,240]{3,2,1,0:T(8,128)} %shard_map.109) | data formatting | bytes 403200 | tf_op jit(solution)/shard_map/pallas_call | solution.py:785

commit v5 on v4

--- a/solution.py
+++ b/solution.py
@@ -609,13 +609,35 @@
     for p in range(1, NPL):
         line = line + pltpu.roll(jnp.where(plane_id == p, planes, 0.0), p * 2 * STK, 1)
     send_v[:, 0, :] = jnp.sum(line.reshape(ng, 8, LANES), axis=1)
-    recv_v[j] = send_v[j]
-
-    def copy_v(k):
-        return copy_ga(send_v.at[lax.rem(j + k, ng)], recv_v.at[j], v_ssem, v_rsem, k)
-
-    for k in range(1, ng):
-        copy_v(k).start()
+    straight = (5, -5, 0, 1, -1, 2, -2) if nb == 16 else tuple(range(nb))
+    rows_sent = [ng - 1 if off == 0 else ng for off in straight]
+    recv_v[straight.index(0), j] = send_v[j]
+
+    def copy_v(n, k):
+        place = lax.rem(j + k, ng)
+        return pltpu.make_async_remote_copy(
+            send_v.at[place],
+            recv_v.at[n, j],
+            v_ssem.at[n],
+            v_rsem.at[n],
+            device_id=(lax.rem(b + nb + straight[n], nb), place),
+            device_id_type=MESH,
+        )
+
+    def copy_rows(n):
+        rows = recv_v.at[n, pl.ds(0, rows_sent[n])]
+        return pltpu.make_async_remote_copy(
+            rows,
+            rows,
+            v_ssem.at[n],
+            v_rsem.at[n],
+            device_id=(lax.rem(b + nb + 1, nb), j),
+            device_id_type=MESH,
+        )
+
+    for n, off in enumerate(straight):
+        for k in range(ng - rows_sent[n], ng):
+            copy_v(n, k).start()
 
     def end_band(k):
         off = band_offset(k)
@@ -623,7 +645,6 @@
 
     def end_ga(k):
         copy_ga(send_a, recv_a.at[j], a_ssem, a_rsem, k).wait_send()
-        copy_v(k).wait_send()
 
     def wait_keys(k):
         off = band_offset(k)
@@ -659,14 +680,12 @@
 
     loop(0, nb * (slots // some_rows), y_phases)
     loop(0, nb - 1, end_band)
-    loop(1, ng, lambda k: copy_v(k).wait_recv())
-
+    loop(1, ng, end_ga)
+
+    hops = {}
     if nb == 16:
-        hops = {n: (0, n) for n in (5, -5, 1, -1, 2, -2)}
-        hops.update({5 + n: (5, n) for n in (3, 2, -2, 1, -1)})
+        hops = {5 + n: (5, n) for n in (3, 2, -2, 1, -1)}
         hops.update({-5 + n: (-5, n) for n in (2, -2, 1, -1)})
-    else:
-        hops = {n: (0, n) for n in range(1, nb)}
 
     def copy_y(off):
         back, hop = hops[off]
@@ -685,10 +704,6 @@
             if hops[off][0] == back:
                 copy_y(off).start()
 
-    recv_y[b] = recv_v[:, 0, :]
-    pass_on(0)
-    loop(1, ng, end_ga)
-
     group = lax.broadcasted_iota(jnp.int32, (2 * ng, LANES), 1) // 16 * 16
 
     def take_blocks(sources):
@@ -703,14 +718,34 @@
             rows = pl.ds(pl.multiple_of(source * 16, 16), 16)
             field[rows, :] = dot_nn(onehot[source], jnp.concatenate(split(z), axis=0))
 
-    take_blocks([b])
-    groups_of = [(5, -5), (1, -1, 2, -2), (3, -3, 4, -4, 6, -6, 7, -7, 8)]
-    for offs in groups_of if nb == 16 else [(n,) for n in range(1, nb)]:
-        for off in offs:
-            copy_y(off).wait_recv()
+    def source_of(off):
+        return lax.rem(b + nb - off, nb)
+
+    def arrived(off):
+        n = straight.index(off)
+        copy_rows(n).wait_recv()
+        recv_y[source_of(off)] = recv_v[n, :, 0, :]
+
+    def take_all(offs):
+        for n in range(0, len(offs), 2):
+            take_blocks([source_of(off) for off in offs[n : n + 2]])
+
+    if nb == 16:
+        arrived(0)
+        take_all((0,))
+        for off in (5, -5):
+            arrived(off)
             pass_on(off)
-        for n in range(0, len(offs), 2):
-            take_blocks([(b + nb - off) % nb for off in offs[n : n + 2]])
+        for off in (1, -1, 2, -2):
+            arrived(off)
+        take_all((5, -5, 1, -1, 2, -2))
+    else:
+        for off in straight:
+            arrived(off)
+        take_all(straight)
+    for off in hops:
+        copy_y(off).wait_recv()
+    take_all(tuple(hops))
 
     turned = field[...].T
     f_re, f_im = turned[:LANES], turned[LANES:]
@@ -727,6 +762,8 @@
 
     for off in hops:
         copy_y(off).wait_send()
+    for n in range(len(straight)):
+        copy_rows(n).wait_send()
 
 
 def both_parts(table):
@@ -822,7 +859,7 @@
             pltpu.VMEM((2 * atoms, KLANES), BF16),
             pltpu.VMEM((8, round_up(columns, LANES)), F32),
             pltpu.VMEM((ng, 1, LANES), F32),
-            pltpu.VMEM((ng, 1, LANES), F32),
+            pltpu.VMEM((min(nb, 7), ng, 1, LANES), F32),
             pltpu.VMEM((nb, ng, LANES), F32),
             pltpu.VMEM((nb, 2, slots, LANES), F32),
             pltpu.VMEM((nb, 16, 2 * slots), BF16),

time: 66.9 us -> 66.1 us (0.988)
  Pallas kernels: 64.9 us -> 64.2 us
    pallas_call x1, Pallas kernels: 64.9 us -> 64.2 us  [on_device(): pl.pallas_call(functools.partial(kernel, nb, ng, gt_lanes), out_shape=jax...]
where the time goes in v5:
time: 66.1 us; the launch traced here: 66 us
  Pallas kernels  64.2 us (97%)
  local copies, waits for them, and re-layouts  1.79 us (3%)
    pallas_call x1, Pallas kernels, on_device(): pl.pallas_call(functools.partial(kernel, nb, ng, gt_lanes), out_shape=jax...  64.2 us
    pallas_call x1, local copies, waits for them, and re-layouts, on_device(): pl.pallas_call(functools.partial(kernel, nb, ng, gt_lanes), out_shape=jax...  1.79 us

profile of v5, /device:TPU:1, one launch (start us, length us, event | category | flops | bytes accessed | tf_op | source)
XLA Modules:
  0.0 66.0 jit_solution(10380205479447507446)
XLA Ops:
  0.0 64.2 %shard_map.109 = f32[2,7,15,240]{3,2,1,0:T(8,128)} custom-call(bf16[2,32,1024]{2,1,0:T(8,128)(2,1)} %waves_hbm.1, f32[1,32]{1,0:T(1,128)} %bitcast.3, f32[72,1024]{1,0:T(8,128)} %beta_hbm.1, s32[3,1024]{1,0:T(4,128)} %mil_hbm.1, s32[1,256]{1,0:T(1,128)} %bitcast.2, s32[3,256]{1,0:T(4,128)} %sites_hbm.1, bf16[684,1792]{1,0:T(8,128)(2,1)} %tab_hbm.1, ...), custom_call_target="tpu_custom_call" | custom-call | tf_op jit(solution)/shard_map/pallas_call | solution.py:822
  64.2 1.8 %copy.12 = f32[2,7,15,240]{3,0,2,1:T(2,128)} copy(f32[2,7,15,240]{3,2,1,0:T(8,128)} %shard_map.109) | data formatting | bytes 403200 | tf_op jit(solution)/shard_map/pallas_call | solution.py:822
